TPU v7x, 32 devices: a whole 2x2x4 slice. The times are simulated.
32 devices in a mesh: dp: 2 (over x), tp: 4 (over z), sp: 4 (over y, core).
Axes of the slice: x: 2, y: 2, z: 4, core: 2. Of those that a mesh axis runs over, the one named last changes fastest.
Arguments:
- layer_in: bfloat16 [128, 5120], P('dp'), parts along dimension 0
- new_pos: int32 [128], P('dp'), parts along dimension 0
- k_cache: bfloat16 [128, 512, 8, 128], P('dp', 'sp', 'tp'), parts along dimension 0
- v_cache: bfloat16 [128, 512, 8, 128], P('dp', 'sp', 'tp'), parts along dimension 0
- attn_gain: bfloat16 [5120], replicated
- w_query: bfloat16 [5120, 4096], P(None, 'tp')
- w_key: bfloat16 [5120, 1024], P(None, 'tp')
- w_value: bfloat16 [5120, 1024], P(None, 'tp')
- w_out: bfloat16 [4096, 5120], P('tp')
- mlp_gain: bfloat16 [5120], replicated
- w_gate: bfloat16 [5120, 14336], P(None, 'tp')
- w_up: bfloat16 [5120, 14336], P(None, 'tp')
- w_down: bfloat16 [14336, 5120], P('tp')
Outputs:
- output 1: bfloat16 [128, 5120], P('dp'), parts along dimension 0
- output 2: bfloat16 [128, 512, 8, 128], P('dp', 'sp', 'tp'), parts along dimension 0
- output 3: bfloat16 [128, 512, 8, 128], P('dp', 'sp', 'tp'), parts along dimension 0
- output 4: bfloat16 [128, 8, 128], P('dp', 'tp'), parts along dimension 0
- output 5: bfloat16 [128, 8, 128], P('dp', 'tp'), parts along dimension 0
There are 2 independent parts. A program takes and returns all parts, laid end to end along the dimension named above; an argument that names none is the same for every part.
All inputs are finite; a program needn't handle non-finite values.
Results may differ from a plain program's by a relative error of at most 0.0049299.
Values sent between devices are 32-bit elements.
A program may use at most 1 GiB of HBM per device.

v0:
```python
import jax
import jax.numpy as jnp
from jax import lax
from jax.sharding import PartitionSpec as P

ROPE_THETA = 1000000


def rms_norm(in_vec, gain_vec):
    mean_sq = jnp.mean(jnp.square(in_vec), axis=-1, keepdims=True)
    return in_vec * lax.rsqrt(mean_sq + 1e-5) * gain_vec.astype(jnp.float32)


def apply_rotary(in_vec, positions):
    head_dim = in_vec.shape[-1]
    half_idx = jnp.arange(head_dim // 2, dtype=jnp.float32)
    inv_freq = 1.0 / (ROPE_THETA ** (2.0 * half_idx / head_dim))
    angles = positions.astype(jnp.float32)[:, None] * inv_freq[None, :]
    cos_a = jnp.cos(angles)[:, None, :]
    sin_a = jnp.sin(angles)[:, None, :]
    pair_view = in_vec.reshape(in_vec.shape[:-1] + (head_dim // 2, 2))
    even_part = pair_view[..., 0]
    odd_part = pair_view[..., 1]
    rotated = jnp.stack([even_part * cos_a - odd_part * sin_a, even_part * sin_a + odd_part * cos_a], axis=-1)
    return rotated.reshape(in_vec.shape)


def solution(mesh):
    def local_step(layer_in, new_pos, k_blk, v_blk, attn_gain, w_query, w_key, w_value, w_out, mlp_gain, w_gate, w_up, w_down):
        num_rows = layer_in.shape[0]
        blk_len = k_blk.shape[1]
        kv_loc = k_blk.shape[2]
        head_dim = k_blk.shape[3]
        heads_loc = w_query.shape[1] // head_dim
        group_size = heads_loc // kv_loc
        x_f32 = layer_in.astype(jnp.float32)
        normed = rms_norm(x_f32, attn_gain).astype(jnp.bfloat16)
        q_proj = jnp.dot(normed, w_query, preferred_element_type=jnp.float32).reshape(num_rows, heads_loc, head_dim)
        k_proj = jnp.dot(normed, w_key, preferred_element_type=jnp.float32).reshape(num_rows, kv_loc, head_dim)
        v_new = jnp.dot(normed, w_value, preferred_element_type=jnp.float32).reshape(num_rows, kv_loc, head_dim).astype(jnp.bfloat16)
        q_rot = apply_rotary(q_proj, new_pos).astype(jnp.bfloat16)
        k_rot = apply_rotary(k_proj, new_pos).astype(jnp.bfloat16)
        slot_ids = lax.axis_index('sp') * blk_len + jnp.arange(blk_len)
        is_new = (slot_ids[None, :] == new_pos[:, None])[:, :, None, None]
        k_upd = jnp.where(is_new, k_rot[:, None], k_blk)
        v_upd = jnp.where(is_new, v_new[:, None], v_blk)
        q_grp = q_rot.reshape(num_rows, kv_loc, group_size, head_dim)
        scores = jnp.einsum('bkgd,bskd->bkgs', q_grp, k_upd, preferred_element_type=jnp.float32) * (head_dim ** -0.5)
        is_valid = (slot_ids[None, :] <= new_pos[:, None])[:, None, None, :]
        scores = jnp.where(is_valid, scores, -jnp.inf)
        row_max = lax.pmax(jnp.max(scores, axis=-1, keepdims=True), 'sp')
        prob_vals = jnp.exp(scores - row_max)
        denom_sum = lax.psum(jnp.sum(prob_vals, axis=-1, keepdims=True), 'sp')
        part_vals = jnp.einsum('bkgs,bskd->bkgd', prob_vals.astype(jnp.bfloat16), v_upd, preferred_element_type=jnp.float32)
        weighted = lax.psum(part_vals, 'sp')
        attn_vec = (weighted / denom_sum).reshape(num_rows, heads_loc * head_dim).astype(jnp.bfloat16)
        hidden = x_f32 + lax.psum(jnp.dot(attn_vec, w_out, preferred_element_type=jnp.float32), 'tp')
        normed_mlp = rms_norm(hidden, mlp_gain).astype(jnp.bfloat16)
        gate_pre = jnp.dot(normed_mlp, w_gate, preferred_element_type=jnp.float32)
        up_proj = jnp.dot(normed_mlp, w_up, preferred_element_type=jnp.float32)
        act_bf = (jax.nn.silu(gate_pre) * up_proj).astype(jnp.bfloat16)
        mlp_part = jnp.dot(act_bf, w_down, preferred_element_type=jnp.float32)
        layer_out = (hidden + lax.psum(mlp_part, 'tp')).astype(jnp.bfloat16)
        return layer_out, k_upd, v_upd, k_rot, v_new

    cache_spec = P('dp', 'sp', 'tp', None)
    new_spec = P('dp', 'tp', None)
    in_specs = (P('dp', None), P('dp'), cache_spec, cache_spec, P(None), P(None, 'tp'), P(None, 'tp'), P(None, 'tp'), P('tp', None), P(None), P(None, 'tp'), P(None, 'tp'), P('tp', None))
    out_specs = (P('dp', None), cache_spec, cache_spec, new_spec, new_spec)
    return jax.shard_map(local_step, mesh=mesh, in_specs=in_specs, out_specs=out_specs, check_vma=False)
```

profile of v0, /device:TPU:1, one launch (start us, length us, event | category | flops | bytes accessed | tf_op | source)
XLA Modules:
  0.0 273.7 jit_solution(653151501980399568)
XLA Ops:
  7.2 0.0 copy-start
  7.2 0.0 copy-start.2
  7.2 0.0 all-reduce.4.cloned.1.call-start
  7.3 0.8 convert_element_type.60
  8.1 1.4 fusion.6
  9.5 0.7 broadcast_compare_fusion.1
  10.3 0.7 convert_element_type.58
  11.0 0.0 copy-done
  11.0 1.7 convolution_convert_fusion
  12.7 0.0 copy-done.2
  12.7 0.0 copy-start.6
  12.7 2.9 %fusion.27 = f32[64,256]{0,1:T(8,128)S(1)} fusion(bf16[5120,256]{1,0:T(8,128)(2,1)} %param.19, bf16[64,5120]{1,0:T(8,128)(2,1)S(1)} %copy-done.2, f32[5120]{0:T(1024)S(1)} %convert_element_type.58, f32[64]{0:T(128)S(1)} %add_rsqrt_fusion.1), kind=kOutput, calls=%fused_computation.47 | convolution fusion | flops 169082880 | bytes 3363072 | tf_op jit(solution)/shard_map/dot_general | solution.py:39
  15.6 0.2 multiply_cosine_fusion
  15.8 0.2 subtract_convert_fusion.1
  16.0 0.2 pad_maximum_fusion.1
  16.2 0.1 copy.22
  16.3 0.0 copy-start.5
  16.3 7.0 %fusion.29 = f32[64,1024]{0,1:T(8,128)S(1)} fusion(bf16[5120,1024]{1,0:T(8,128)(2,1)} %param.18, bf16[64,5120]{1,0:T(8,128)(2,1)S(1)} %copy-done.2, f32[5120]{0:T(1024)S(1)} %convert_element_type.58, f32[64]{0:T(128)S(1)} %add_rsqrt_fusion.1), kind=kOutput, calls=%fused_computation.48 | convolution fusion | flops 672399360 | bytes 11424000 | tf_op jit(solution)/shard_map/dot_general | solution.py:38
  23.4 0.7 subtract_convert_fusion
  24.0 0.7 pad_maximum_fusion
  24.7 0.2 copy.23
  24.9 0.0 copy-done.6
  24.9 0.0 copy-done.5
  24.9 13.7 %broadcast_select_fusion.1 = (bf16[64,128,2,128]{3,2,1,0:T(2,128)(2,1)S(1)}, bf16[64,128,2,128]{3,2,1,0:T(2,128)(2,1)}) fusion(bf16[64,128,2,128]{3,2,1,0:T(2,128)(2,1)} %param.15, pred[64,128]{1,0:T(8,128)(4,1)S(1)} %get-tuple-element.17, bf16[64,2,128]{2,1,0:T(2,128)(2,1)S(1)} %copy.22, bf16[64,128,2,128]{3,2,1,0:T(2,128)(2,1)} %param.16, ...), kind=kLoop, calls=%fused_computation.1 | loop fusion | flops 4194304 | bytes 16850944 | tf_op jit(solution)/shard_map/jit(_where)/select_n | solution.py:45
  38.6 0.0 copy-start.4
  38.6 2.0 copy-done.4
  40.6 2.4 fusion.31
  43.1 11.6 %pmax.7 = f32[64,2,4]{2,1,0:T(2,128)S(1)} all-reduce(f32[64,2,4]{2,1,0:T(2,128)S(1)} %get-tuple-element.20), channel_id=1, replica_groups=mesh['dp'=2,'tp'=4,'sp'=4] {'sp'}, use_global_device_ids=true, to_apply=%region_2.3 | all-reduce | flops 512 | bytes 4096 | tf_op jit(solution)/shard_map/pmax | solution.py:51
  54.7 4.1 %fusion.1 = f32[64,2,4,128]{3,2,1,0:T(4,128)} fusion(bf16[64,128,2,128]{3,2,1,0:T(2,128)(2,1)} %get-tuple-element.15, f32[64,2,4,128]{3,2,1,0:T(4,128)S(1)} %get-tuple-element.21, f32[64,2,4]{2,1,0:T(2,128)S(1)} %pmax.7), kind=kOutput, calls=%fused_computation.4 | convolution fusion | flops 16908288 | bytes 4720640 | tf_op jit(solution)/shard_map/bkgs,bskd->bkgd/dot_general | solution.py:54
  58.8 0.0 all-reduce.4.cloned.1.call-update
  58.9 0.0 all-reduce.6.cloned.1.call-start
  58.9 0.4 fusion.21
  59.3 12.2 %psum.29 = f32[64,2,4]{2,1,0:T(2,128)S(1)} all-reduce(f32[64,2,4]{2,1,0:T(2,128)S(1)} %fusion.21), channel_id=1, replica_groups=mesh['dp'=2,'tp'=4,'sp'=4] {'sp'}, use_global_device_ids=true, to_apply=%region_5.6 | all-reduce | flops 512 | bytes 4096 | tf_op jit(solution)/shard_map/psum | solution.py:53
  71.5 19.6 %all-reduce.4.cloned.1.call-done = f32[64,2,4,128]{3,2,1,0:T(4,128)} async-done(((f32[64,2,4,128]{3,2,1,0:T(4,128)}), f32[64,2,4,128]{3,2,1,0:T(4,128)}) %all-reduce.4.cloned.1.call-update) | async-done | bytes 262160 | tf_op jit(solution)/shard_map/psum | solution.py:55
  91.2 1.2 divide_convert_fusion
  92.3 0.1 convert_element_type.67
  92.4 0.0 copy-start.7
  92.4 7.0 %fusion.32 = f32[64,5120]{1,0:T(8,128)} fusion(bf16[64,1024]{1,0:T(8,128)(2,1)S(1)} %convert_element_type.67, bf16[1024,5120]{1,0:T(8,128)(2,1)} %param.21), kind=kOutput, calls=%fused_computation.50 | convolution fusion | flops 671088640 | bytes 11927552 | tf_op jit(solution)/shard_map/dot_general | solution.py:57
  99.4 0.0 all-reduce.6.cloned.1.call-update
  99.4 0.2 all-reduce.8.cloned.1.call-start
  99.7 61.8 %all-reduce.6.cloned.1.call-done = f32[64,5120]{1,0:T(8,128)} async-done(((f32[64,5120]{1,0:T(8,128)}), f32[64,5120]{1,0:T(8,128)}) %all-reduce.6.cloned.1.call-update) | async-done | bytes 1310736 | tf_op jit(solution)/shard_map/psum | solution.py:57
  161.5 1.7 multiply_reduce_fusion
  163.2 0.2 multiply_convert_fusion
  163.4 14.7 %fusion.33 = f32[64,3584]{1,0:T(8,128)S(1)} fusion(bf16[64,5120]{1,0:T(8,128)(2,1)S(1)} %multiply_convert_fusion, bf16[5120,3584]{1,0:T(8,128)(2,1)} %param.23), kind=kOutput, calls=%fused_computation.51 | convolution fusion | flops 2348810240 | bytes 38273024 | tf_op jit(solution)/shard_map/dot_general | solution.py:59
  178.1 26.5 %fusion.5 = f32[64,5120]{1,0:T(8,128)} fusion(bf16[3584,5120]{1,0:T(8,128)(2,1)} %param.25, bf16[64,5120]{1,0:T(8,128)(2,1)S(1)} %multiply_convert_fusion, bf16[5120,3584]{1,0:T(8,128)(2,1)} %param.24, f32[64,3584]{1,0:T(8,128)S(1)} %fusion.33), kind=kOutput, calls=%fused_computation.8 | convolution fusion | flops 4698996736 | bytes 76283904 | tf_op jit(solution)/shard_map/dot_general | solution.py:62
  204.6 0.0 all-reduce.8.cloned.1.call-update
  204.6 59.9 %all-reduce.8.cloned.1.call-done = f32[64,5120]{1,0:T(8,128)} async-done(((f32[64,5120]{1,0:T(8,128)}), f32[64,5120]{1,0:T(8,128)}) %all-reduce.8.cloned.1.call-update) | async-done | bytes 1310736 | tf_op jit(solution)/shard_map/psum | solution.py:63
  264.5 2.7 add_convert_fusion
  (11 shorter events, 0.1 us)
Async XLA Ops:
  7.2 3.8 %copy-start = (bf16[5120,256]{1,0:T(8,128)(2,1)S(1)}, bf16[5120,256]{1,0:T(8,128)(2,1)}, u32[]{:S(2)}) copy-start(bf16[5120,256]{1,0:T(8,128)(2,1)} %param.20) | copy-start | bytes 7864324
  7.2 5.5 %copy-start.2 = (bf16[64,5120]{1,0:T(8,128)(2,1)S(1)}, bf16[64,5120]{1,0:T(8,128)(2,1)}, u32[]{:S(2)}) copy-start(bf16[64,5120]{1,0:T(8,128)(2,1)} %param.13) | copy-start | bytes 1966084
  7.2 84.0 %all-reduce.4.cloned.1.call-start = ((), (), s32[]{:S(2)}) async-start(), calls=%async_computation | async-start | bytes 524288 | tf_op jit(solution)/shard_map/psum | solution.py:55
  12.7 12.2 %copy-start.6 = (bf16[64,2,128]{2,1,0:T(2,128)(2,1)}, bf16[64,2,128]{2,1,0:T(2,128)(2,1)S(1)}, u32[]{:S(2)}) copy-start(bf16[64,2,128]{2,1,0:T(2,128)(2,1)S(1)} %convert_element_type.65) | copy-start | bytes 98308
  16.3 8.6 %copy-start.5 = (bf16[64,2,128]{2,1,0:T(2,128)(2,1)}, bf16[64,2,128]{2,1,0:T(2,128)(2,1)S(1)}, u32[]{:S(2)}) copy-start(bf16[64,2,128]{2,1,0:T(2,128)(2,1)S(1)} %copy.22) | copy-start | bytes 98308
  38.6 2.0 copy-start.4
  58.9 102.6 %all-reduce.6.cloned.1.call-start = ((), (), s32[]{:S(2)}) async-start(), calls=%async_computation.1 | async-start | bytes 2621440 | tf_op jit(solution)/shard_map/psum | solution.py:57
  92.4 7.3 %copy-start.7 = (bf16[5120]{0:T(1024)(128)(2,1)S(1)}, bf16[5120]{0:T(1024)(128)(2,1)}, u32[]{:S(2)}) copy-start(bf16[5120]{0:T(1024)(128)(2,1)} %param.22) | copy-start | bytes 30724
  99.4 165.1 %all-reduce.8.cloned.1.call-start = ((), (), s32[]{:S(2)}) async-start(), calls=%async_computation.2 | async-start | bytes 2621440 | tf_op jit(solution)/shard_map/psum | solution.py:63
  161.4 1.7 copy-start.3
  204.6 62.6 %copy-start.1 = (bf16[5120,256]{1,0:T(8,128)(2,1)S(1)}, bf16[5120,256]{1,0:T(8,128)(2,1)}, u32[]{:S(2)}) copy-start(bf16[5120,256]{1,0:T(8,128)(2,1)} %param.20) | copy-start | bytes 7864324
Sparse Core Ops, SparseCore 0:
  59.0 32.1 all-reduce.3
  99.5 61.8 all-reduce.5
  204.8 59.6 all-reduce.7
where the time goes:
time: 275 us; the launch traced here: 274 us
  waiting for transfers between devices  141 us (51%)
  matrix products  66.4 us (24%)
  other arithmetic  25.5 us (9%)
  blocking collectives  23.8 us (9%)
  between operations  14 us (5%)
    psum x1, waiting for transfers between devices, local_step(): lax.psum(jnp.dot(attn_vec, w_out, preferred_element_type=jnp.float32), 'tp')  61.8 us
    psum x1, waiting for transfers between devices, local_step(): layer_out = (hidden + lax.psum(mlp_part, 'tp')).astype(jnp.bfloat16)  59.9 us
    dot_general x1, matrix products, local_step(): mlp_part = jnp.dot(act_bf, w_down, preferred_element_type=jnp.float32)  26.5 us
    psum x1, waiting for transfers between devices, local_step(): weighted = lax.psum(part_vals, 'sp')  19.6 us
    dot_general x1, matrix products, local_step(): gate_pre = jnp.dot(normed_mlp, w_gate, preferred_element_type=jnp.float32)  14.7 us
    select_n x1, other arithmetic, local_step(): k_upd = jnp.where(is_new, k_rot[:, None], k_blk)  13.7 us
    psum x1, blocking collectives, local_step(): denom_sum = lax.psum(jnp.sum(prob_vals, axis=-1, keepdims=True), 'sp')  12.2 us
    pmax x1, blocking collectives, local_step(): row_max = lax.pmax(jnp.max(scores, axis=-1, keepdims=True), 'sp')  11.6 us
  transfers between devices with their start and end apart: 3, of which 3 were waited for; matrix products, arithmetic and copies ran while one was open for 0% of the time, Pallas kernels for 0%

commit v1 on v0

v1 whole, which is shorter than its diff:
```python
import functools

import jax
import jax.numpy as jnp
import numpy as np
from jax import lax
from jax.experimental import pallas as pl
from jax.experimental.pallas import tpu as pltpu
from jax.sharding import PartitionSpec as P

ROPE_THETA = 1000000
MESH = pl.DeviceIdType.MESH
F32 = jnp.float32
BF16 = jnp.bfloat16
NEG = float(np.finfo(np.float32).min)
VMEM_LIMIT = 62 * 1024 * 1024
ANY = pl.BlockSpec(memory_space=pl.ANY)
VM = pl.BlockSpec(memory_space=pltpu.VMEM)

ROWS = 64
DIM = 5120
HD = 128
HEADS = 8
KV = 2
BLK = 128
QKV = (HEADS + 2 * KV) * HD
KSTEP = 512
KCH = DIM // KSTEP
BCH = 8
NB = ROWS // BCH


def attend_kernel(pos_hbm, x_hbm, gain_hbm, freq_hbm, wq, wk, wv, kc, vc,
                  ko, vo, kn_ref, vn_ref, part_ref,
                  pos_s, x_v, gain_v, freq_v, w_v, k_v, v_v, n_v, acc, pos_v, qs, ks, vs,
                  sem_m, sem_w, sem_k, sem_v, sem_ko, sem_vo):
    sp = lax.axis_index('sp')

    small = [pltpu.make_async_copy(pos_hbm, pos_s, sem_m.at[0]),
             pltpu.make_async_copy(x_hbm, x_v, sem_m.at[1]),
             pltpu.make_async_copy(gain_hbm, gain_v, sem_m.at[2]),
             pltpu.make_async_copy(freq_hbm, freq_v, sem_m.at[3])]
    for cp in small:
        cp.start()

    def w_copies(i):
        rows = pl.ds(pl.multiple_of(i * KSTEP, KSTEP), KSTEP)
        return (pltpu.make_async_copy(wq.at[rows], w_v.at[rows, pl.ds(0, 1024)], sem_w.at[i, 0]),
                pltpu.make_async_copy(wk.at[rows], w_v.at[rows, pl.ds(1024, 256)], sem_w.at[i, 1]),
                pltpu.make_async_copy(wv.at[rows], w_v.at[rows, pl.ds(1280, 256)], sem_w.at[i, 2]))

    def cache_copy(src, dst, sem, i):
        rows = pl.ds(pl.multiple_of(i * BCH, BCH), BCH)
        return pltpu.make_async_copy(src.at[rows], dst.at[rows], sem.at[i])

    for i in range(KCH):
        for cp in w_copies(i):
            cp.start()
    for i in range(NB):
        cache_copy(kc, k_v, sem_k, i).start()
        cache_copy(vc, v_v, sem_v, i).start()

    for cp in small:
        cp.wait()
    for r in range(0, ROWS, 16):
        x = x_v[r:r + 16, :].astype(F32)
        inv = lax.rsqrt(jnp.mean(x * x, axis=-1, keepdims=True) + 1e-5)
        n_v[r:r + 16, :] = (x * inv * gain_v[...].astype(F32)).astype(BF16)
    for b in range(ROWS):
        pos_v[b:b + 1, :] = jnp.full((1, HD), pos_s[b], jnp.int32)
    angles = pos_v[...].astype(F32) * freq_v[...]
    cos_a = jnp.cos(angles)
    sin_a = jnp.sin(angles)
    odd = lax.broadcasted_iota(jnp.int32, (ROWS, HD), 1) % 2 == 1
    sin_a = jnp.where(odd, sin_a, -sin_a)

    acc[...] = jnp.zeros_like(acc)

    def w_step(i, carry):
        for cp in w_copies(i):
            cp.wait()
        rows = pl.ds(pl.multiple_of(i * KSTEP, KSTEP), KSTEP)
        acc[...] += jnp.dot(n_v[:, rows], w_v[rows, :], preferred_element_type=F32)
        return carry

    lax.fori_loop(0, KCH, w_step, 0)

    def rotate(val):
        swapped = jnp.where(odd, pltpu.roll(val, 1, 1), pltpu.roll(val, HD - 1, 1))
        return (val * cos_a + swapped * sin_a).astype(BF16).astype(F32)

    for h in range(HEADS):
        qs[pl.ds(h, ROWS, stride=HEADS), :] = rotate(acc[:, h * HD:(h + 1) * HD])
    for h in range(KV):
        lo = (HEADS + h) * HD
        ks[pl.ds(h, ROWS, stride=KV), :] = rotate(acc[:, lo:lo + HD])
        lo = (HEADS + KV + h) * HD
        vs[pl.ds(h, ROWS, stride=KV), :] = acc[:, lo:lo + HD].astype(BF16).astype(F32)
    kn_ref[...] = ks[...].astype(BF16)
    vn_ref[...] = vs[...].astype(BF16)

    row16 = lax.broadcasted_iota(jnp.int32, (16, HD), 0)
    lane = lax.broadcasted_iota(jnp.int32, (HEADS, KV * BLK), 1)
    group = lax.broadcasted_iota(jnp.int32, (HEADS, KV * BLK), 0) // (HEADS // KV)
    same_head = (lane % KV) == group
    lane_slot = lane // KV
    stat_lane = lax.broadcasted_iota(jnp.int32, (HEADS, HD), 1)

    def put_new(cache_v, new, b, slot):
        inside = jnp.logical_and(slot >= 0, slot < BLK)
        tile = jnp.where(inside, slot // 8, 0)
        local = jnp.where(inside, slot - tile * 8, -1)
        at = pl.ds(pl.multiple_of(tile * 16, 16), 16)
        old = cache_v[b, at, :].astype(F32)
        both = jnp.where(row16 % 2 == 0, new[pl.ds(2 * b, 1), :], new[pl.ds(2 * b + 1, 1), :])
        cache_v[b, at, :] = jnp.where(row16 // 2 == local, both, old).astype(BF16)

    def chunk(i, stat):
        cache_copy(kc, k_v, sem_k, i).wait()
        cache_copy(vc, v_v, sem_v, i).wait()
        slots = [pos_s[i * BCH + u] - sp * BLK for u in range(BCH)]
        for u in range(BCH):
            put_new(k_v, ks, i * BCH + u, slots[u])
            put_new(v_v, vs, i * BCH + u, slots[u])
        cache_copy(k_v, ko, sem_ko, i).start()
        cache_copy(v_v, vo, sem_vo, i).start()
        raw = []
        for u in range(BCH):
            b = i * BCH + u
            q = qs[pl.ds(pl.multiple_of(b * HEADS, HEADS), HEADS), :].astype(BF16)
            raw.append(lax.dot_general(q, k_v[b], (((1,), (1,)), ((), ())), preferred_element_type=F32))
        for u in range(BCH):
            b = i * BCH + u
            valid = jnp.logical_and(same_head, lane_slot <= slots[u])
            score = jnp.where(valid, raw[u] * (HD ** -0.5), NEG)
            top = jnp.max(score, axis=-1, keepdims=True)
            prob = jnp.where(valid, jnp.exp(score - top), 0.0)
            total = jnp.sum(prob, axis=-1, keepdims=True)
            out = jnp.dot(prob.astype(BF16), v_v[b], preferred_element_type=F32)
            half = b // 32
            part_ref[half, pl.ds(pl.multiple_of((b - half * 32) * HEADS, HEADS), HEADS), :] = out
            stat = jnp.where(stat_lane == b, top, stat)
            stat = jnp.where(stat_lane == b + ROWS, total, stat)
        return stat

    stat = lax.fori_loop(0, NB, chunk, jnp.zeros((HEADS, HD), F32))
    part_ref[0, 256:264, :] = stat
    part_ref[1, 256:264, :] = pltpu.roll(stat, 96, 1)
    for i in range(NB):
        cache_copy(k_v, ko, sem_ko, i).wait()
        cache_copy(v_v, vo, sem_vo, i).wait()


def attend(new_pos, x, gain, freq, wq, wk, wv, kc, vc):
    cache = jax.ShapeDtypeStruct(kc.shape, BF16)
    new = jax.ShapeDtypeStruct((ROWS * KV, HD), BF16)
    return pl.pallas_call(
        attend_kernel,
        out_shape=(cache, cache, new, new, jax.ShapeDtypeStruct((2, 264, HD), F32)),
        in_specs=[ANY] * 9,
        out_specs=(ANY, ANY, VM, VM, VM),
        scratch_shapes=[
            pltpu.SMEM((ROWS,), jnp.int32),
            pltpu.VMEM((ROWS, DIM), BF16),
            pltpu.VMEM((1, DIM), F32),
            pltpu.VMEM((1, HD), F32),
            pltpu.VMEM((DIM, QKV), BF16),
            pltpu.VMEM(kc.shape, BF16),
            pltpu.VMEM(vc.shape, BF16),
            pltpu.VMEM((ROWS, DIM), BF16),
            pltpu.VMEM((ROWS, QKV), F32),
            pltpu.VMEM((ROWS, HD), jnp.int32),
            pltpu.VMEM((ROWS * HEADS, HD), F32),
            pltpu.VMEM((ROWS * KV, HD), F32),
            pltpu.VMEM((ROWS * KV, HD), F32),
            pltpu.SemaphoreType.DMA((4,)),
            pltpu.SemaphoreType.DMA((KCH, 3)),
            pltpu.SemaphoreType.DMA((NB,)),
            pltpu.SemaphoreType.DMA((NB,)),
            pltpu.SemaphoreType.DMA((NB,)),
            pltpu.SemaphoreType.DMA((NB,)),
        ],
        compiler_params=pltpu.CompilerParams(vmem_limit_bytes=VMEM_LIMIT),
        name="attend",
    )(new_pos, x, gain, freq, wq, wk, wv, kc, vc)


TP = 4
COLS = DIM // 4
HID = 896
HCH = HID // 128
RB = ROWS // TP
NC = 2
CW = COLS // NC


def mix_kernel(part_ref, x_hbm, gain_hbm, wo, wg, wu, wd, out_ref,
               xb_v, gain_v, wo_v, wgu_v, wd_v,
               pa, pb, pc, at_o, lhs_v, mm, rs_buf, hfull, n2, act, act_b, ofull,
               sem_l, sem_g, sem_d, cs, cr, rs_s, rs_r, az_s, az_r, ay_s, ay_r, ac_s, ac_r,
               my_s, my_r, mc_s, mc_r):
    dp = lax.axis_index('dp')
    z = lax.axis_index('tp')
    sp = lax.axis_index('sp')
    y = sp // 2
    c = sp % 2
    sp_y = (1 - y) * 2 + c
    sp_c = y * 2 + (1 - c)
    sp_yc = (1 - y) * 2 + (1 - c)
    dev_y = (dp, z, sp_y)
    dev_c = (dp, z, sp_c)
    dev_z = [None] + [(dp, lax.rem(z + d, TP), sp) for d in range(1, TP)]
    src_z = [z] + [lax.rem(z + TP - d, TP) for d in range(1, TP)]

    def col_at(s, j=0, width=COLS):
        return pl.ds(pl.multiple_of(s * COLS + j * width, 128), width)

    def row_at(zz):
        return pl.ds(pl.multiple_of(zz * RB, RB), RB)

    loads = [pltpu.make_async_copy(wo.at[:, col_at(sp)], wo_v, sem_l.at[0]),
             pltpu.make_async_copy(x_hbm.at[row_at(z), col_at(sp)], xb_v, sem_l.at[1]),
             pltpu.make_async_copy(gain_hbm, gain_v, sem_l.at[2])]
    for cp in loads:
        cp.start()

    def gu_copies(j):
        cols = pl.ds(pl.multiple_of(sp * HID + j * 128, 128), 128)
        return (pltpu.make_async_copy(wg.at[:, cols], wgu_v.at[j, :, pl.ds(0, 128)], sem_g.at[j, 0]),
                pltpu.make_async_copy(wu.at[:, cols], wgu_v.at[j, :, pl.ds(128, 128)], sem_g.at[j, 1]))

    for j in range(HCH):
        for cp in gu_copies(j):
            cp.start()
    order = [sp, sp_c, sp_y, sp_yc]
    d_copies = [pltpu.make_async_copy(wd.at[pl.ds(pl.multiple_of(s * HID, 128), HID), col_at(sp)],
                                      wd_v.at[i], sem_d.at[i]) for i, s in enumerate(order)]
    for cp in d_copies:
        cp.start()

    barrier = pltpu.get_barrier_semaphore()
    for dev in [dev_y, dev_c] + dev_z[1:]:
        pl.semaphore_signal(barrier, inc=1, device_id=dev, device_id_type=MESH)
    pl.semaphore_wait(barrier, 5)

    sends = []

    def push(src, dst, ssem, rsem, dev):
        cp = pltpu.make_async_remote_copy(src_ref=src, dst_ref=dst, send_sem=ssem, recv_sem=rsem,
                                          device_id=dev, device_id_type=MESH)
        cp.start()
        sends.append(cp)
        return cp

    lane = lax.broadcasted_iota(jnp.int32, (HEADS, HD), 1)

    def weights(s1, s2):
        top = jnp.maximum(s1, s2)
        a1 = jnp.exp(s1 - top)
        a2 = jnp.exp(s2 - top)
        total = a1 * pltpu.roll(s1, 64, 1) + a2 * pltpu.roll(s2, 64, 1)
        return top, a1, a2, total

    cp = push(part_ref.at[1 - c], pa, cs.at[0], cr.at[0], dev_c)
    cp.wait_recv()
    top, a1, a2, total = weights(part_ref[c, 256:264, :], pa[256:264, :])
    for i in range(32):
        r = slice(i * 8, i * 8 + 8)
        pb[r, :] = a1[:, i:i + 1] * part_ref[c, r, :] + a2[:, i:i + 1] * pa[r, :]
    pb[256:264, :] = jnp.where(lane < 64, top, pltpu.roll(total, 64, 1))
    cp = push(pb, pc, cs.at[1], cr.at[1], dev_y)
    cp.wait_recv()
    top, a1, a2, total = weights(pb[256:264, :], pc[256:264, :])
    a1 = a1 / total
    a2 = a2 / total
    half = pl.multiple_of(c * 256, 256)
    for i in range(32):
        r = slice(i * 8, i * 8 + 8)
        at_o[pl.ds(pl.multiple_of(half + i * 8, 8), 8), :] = a1[:, i:i + 1] * pb[r, :] + a2[:, i:i + 1] * pc[r, :]
    mine = at_o.at[pl.ds(half, 256)]
    cp = push(mine, mine, cs.at[2], cr.at[2], dev_c)
    cp.wait_recv()
    for h in range(HEADS):
        lhs_v[:, h * HD:(h + 1) * HD] = at_o[pl.ds(h, ROWS, stride=HEADS), :].astype(BF16)

    def scatter(stage, j):
        cols = pl.ds(j * CW, CW)
        for d in range(1, TP):
            zz = lax.rem(z + d, TP)
            push(mm.at[stage, row_at(zz), cols], rs_buf.at[stage, d - 1, :, cols],
                 rs_s.at[stage, j, d - 1], rs_r.at[stage, j, d - 1], dev_z[d])

    def gather(stage, base, full):
        def blk(s, d, j):
            return full.at[row_at(src_z[d]), col_at(s, 0, COLS) if False else pl.ds(
                pl.multiple_of(s * COLS + j * CW, 128), CW)]

        def wait_in(ref, sem):
            pltpu.make_async_copy(ref, ref, sem).wait()

        for j in range(NC):
            cols = slice(j * CW, (j + 1) * CW)
            val = base(cols) + mm[stage, row_at(z), cols]
            for d in range(1, TP):
                wait_in(rs_buf.at[stage, d - 1, :, pl.ds(j * CW, CW)], rs_r.at[stage, j, d - 1])
                val = val + rs_buf[stage, d - 1, :, cols]
            full[row_at(z), pl.ds(pl.multiple_of(sp * COLS + j * CW, 128), CW)] = val
            own = blk(sp, 0, j)
            for d in range(1, TP):
                push(own, own, az_s.at[stage, j, d - 1], az_r.at[stage, j, d - 1], dev_z[d])
            push(own, own, ay_s.at[stage, j, 0], ay_r.at[stage, j, 0], dev_y)
            push(own, own, ac_s.at[stage, j, 0], ac_r.at[stage, j, 0], dev_c)
        for j in range(NC):
            for d in (1, 3, 2):
                ref = blk(sp, d, j)
                wait_in(ref, az_r.at[stage, j, d - 1])
                push(ref, ref, ay_s.at[stage, j, d], ay_r.at[stage, j, d], dev_y)
                push(ref, ref, ac_s.at[stage, j, d], ac_r.at[stage, j, d], dev_c)
        for j in range(NC):
            for d in (0, 1, 3, 2):
                ref = blk(sp_y, d, j)
                wait_in(ref, ay_r.at[stage, j, d])
                push(ref, ref, ac_s.at[stage, j, TP + d], ac_r.at[stage, j, TP + d], dev_c)
        for j in range(NC):
            for d in range(TP):
                wait_in(blk(sp_c, d, j), ac_r.at[stage, j, d])
                wait_in(blk(sp_yc, d, j), ac_r.at[stage, j, TP + d])

    for cp in loads:
        cp.wait()
    for j in range(NC):
        cols = slice(j * CW, (j + 1) * CW)
        mm[0, :, cols] = jnp.dot(lhs_v[...], wo_v[:, cols], preferred_element_type=F32)
        scatter(0, j)
    gather(0, lambda cols: xb_v[:, cols].astype(F32), hfull)

    for r in range(0, ROWS, 16):
        h = hfull[r:r + 16, :]
        inv = lax.rsqrt(jnp.mean(h * h, axis=-1, keepdims=True) + 1e-5)
        n2[r:r + 16, :] = (h * inv * gain_v[...].astype(F32)).astype(BF16)

    def act_copies(j):
        own = act.at[sp, j]
        return (pltpu.make_async_remote_copy(src_ref=own, dst_ref=own, send_sem=my_s.at[j], recv_sem=my_r.at[j],
                                             device_id=dev_y, device_id_type=MESH),
                pltpu.make_async_remote_copy(src_ref=own, dst_ref=own, send_sem=mc_s.at[0, j], recv_sem=mc_r.at[0, j],
                                             device_id=dev_c, device_id_type=MESH))

    def fwd_copy(j):
        ref = act.at[sp_y, j]
        return pltpu.make_async_remote_copy(src_ref=ref, dst_ref=ref, send_sem=mc_s.at[1, j], recv_sem=mc_r.at[1, j],
                                            device_id=dev_c, device_id_type=MESH)

    def hidden_step(j, carry):
        for cp in gu_copies(j):
            cp.wait()
        gu = jnp.dot(n2[...], wgu_v[j], preferred_element_type=F32)
        gate = gu[:, :128]
        val = gate * jax.nn.sigmoid(gate) * gu[:, 128:]
        act[sp, j] = val.astype(BF16).astype(F32)
        for cp in act_copies(j):
            cp.start()
        return carry

    lax.fori_loop(0, HCH, hidden_step, 0)

    def down(i, s):
        for j in range(HCH):
            act_b[:, j * 128:(j + 1) * 128] = act[s, j].astype(BF16)
        d_copies[i].wait()
        for k in range(0, COLS, 256):
            prod = jnp.dot(act_b[...], wd_v[i, :, k:k + 256], preferred_element_type=F32)
            if i == 0:
                mm[1, :, k:k + 256] = prod
            else:
                mm[1, :, k:k + 256] += prod

    down(0, sp)
    for j in range(HCH):
        act_copies(j)[1].wait_recv()
    down(1, sp_c)
    for j in range(HCH):
        act_copies(j)[0].wait_recv()
        fwd_copy(j).start()
    down(2, sp_y)
    for j in range(HCH):
        fwd_copy(j).wait_recv()
    down(3, sp_yc)
    for j in range(NC):
        scatter(1, j)

    own_h = hfull.at[row_at(z), col_at(sp)]
    gather(1, lambda cols: own_h[:, cols], ofull)
    out_ref[...] = ofull[...].astype(BF16)

    for cp in sends:
        cp.wait_send()
    for j in range(HCH):
        for cp in act_copies(j):
            cp.wait_send()
        fwd_copy(j).wait_send()


def mix(part, x, gain, wo, wg, wu, wd):
    dma = pltpu.SemaphoreType.DMA
    return pl.pallas_call(
        mix_kernel,
        out_shape=jax.ShapeDtypeStruct((ROWS, DIM), BF16),
        in_specs=[VM] + [ANY] * 6,
        out_specs=VM,
        scratch_shapes=[
            pltpu.VMEM((RB, COLS), BF16),
            pltpu.VMEM((1, DIM), F32),
            pltpu.VMEM((1024, COLS), BF16),
            pltpu.VMEM((HCH, DIM, 256), BF16),
            pltpu.VMEM((4, HID, COLS), BF16),
            pltpu.VMEM((264, HD), F32),
            pltpu.VMEM((264, HD), F32),
            pltpu.VMEM((264, HD), F32),
            pltpu.VMEM((ROWS * HEADS, HD), F32),
            pltpu.VMEM((ROWS, 1024), BF16),
            pltpu.VMEM((2, ROWS, COLS), F32),
            pltpu.VMEM((2, TP - 1, RB, COLS), F32),
            pltpu.VMEM((ROWS, DIM), F32),
            pltpu.VMEM((ROWS, DIM), BF16),
            pltpu.VMEM((4, HCH, ROWS, 128), F32),
            pltpu.VMEM((ROWS, HID), BF16),
            pltpu.VMEM((ROWS, DIM), F32),
            dma((3,)), dma((HCH, 2)), dma((4,)),
            dma((3,)), dma((3,)),
            dma((2, NC, 3)), dma((2, NC, 3)),
            dma((2, NC, 3)), dma((2, NC, 3)),
            dma((2, NC, TP)), dma((2, NC, TP)),
            dma((2, NC, 2 * TP)), dma((2, NC, 2 * TP)),
            dma((HCH,)), dma((HCH,)),
            dma((2, HCH)), dma((2, HCH)),
        ],
        compiler_params=pltpu.CompilerParams(vmem_limit_bytes=VMEM_LIMIT, collective_id=0, has_side_effects=True),
        name="mix",
    )(part, x, gain, wo, wg, wu, wd)


def solution(mesh):
    def local_step(layer_in, new_pos, k_blk, v_blk, attn_gain, w_query, w_key, w_value, w_out, mlp_gain, w_gate, w_up, w_down):
        half_idx = np.arange(HD // 2, dtype=np.float32)
        inv_freq = (1.0 / (np.float32(ROPE_THETA) ** (np.float32(2.0) * half_idx / np.float32(HD)))).astype(np.float32)
        freq = jnp.asarray(np.repeat(inv_freq, 2)[None, :])
        flat = (ROWS, BLK * KV, HD)
        k_out, v_out, k_new, v_new, part = attend(
            new_pos, layer_in, attn_gain.astype(F32).reshape(1, DIM), freq, w_query, w_key, w_value,
            k_blk.reshape(flat), v_blk.reshape(flat))
        layer_out = mix(part, layer_in, mlp_gain.astype(F32).reshape(1, DIM), w_out, w_gate, w_up, w_down)
        return (layer_out, k_out.reshape(k_blk.shape), v_out.reshape(v_blk.shape),
                k_new.reshape(ROWS, KV, HD), v_new.reshape(ROWS, KV, HD))

    cache_spec = P('dp', 'sp', 'tp', None)
    new_spec = P('dp', 'tp', None)
    in_specs = (P('dp', None), P('dp'), cache_spec, cache_spec, P(None), P(None, 'tp'), P(None, 'tp'), P(None, 'tp'), P('tp', None), P(None), P(None, 'tp'), P(None, 'tp'), P('tp', None))
    out_specs = (P('dp', None), cache_spec, cache_spec, new_spec, new_spec)
    return jax.shard_map(local_step, mesh=mesh, in_specs=in_specs, out_specs=out_specs, check_vma=False)
```

time: 275 us -> 90.3 us (0.33)
  waiting for transfers between devices: 141 us -> 0 us
  Pallas kernels: 0 us -> 84.4 us
  matrix products: 66.4 us -> 0 us
  blocking collectives: 23.8 us -> 0 us
  other arithmetic: 25.5 us -> 2.61 us
  between operations: 14 us -> 0.65 us
    psum x3 -> x0, waiting for transfers between devices: 141 us -> none  [the longest x1 61.8 us: local_step(): lax.psum(jnp.dot(attn_vec, w_out, preferred_element_type=jnp.float32), 'tp')]
    pallas_call x0 -> x2, Pallas kernels: none -> 84.4 us  [the longest x1 66.1 us: mix(): pl.pallas_call(mix_kernel, out_shape=jax.ShapeDtypeStruct((ROWS, DIM), BF...]
    dot_general x8 -> x0, matrix products: 66.4 us -> none  [the longest x1 26.5 us: local_step(): mlp_part = jnp.dot(act_bf, w_down, preferred_element_type=jnp.float32)]
    select_n x1 -> x0, other arithmetic: 13.7 us -> none  [local_step(): k_upd = jnp.where(is_new, k_rot[:, None], k_blk)]
    psum x1 -> x0, blocking collectives: 12.2 us -> none  [local_step(): denom_sum = lax.psum(jnp.sum(prob_vals, axis=-1, keepdims=True), 'sp')]
    pmax x1 -> x0, blocking collectives: 11.6 us -> none  [local_step(): row_max = lax.pmax(jnp.max(scores, axis=-1, keepdims=True), 'sp')]
    convert_element_type x6 -> x0, other arithmetic: 5.62 us -> none  [the longest x1 2.71 us: local_step(): layer_out = (hidden + lax.psum(mlp_part, 'tp')).astype(jnp.bfloat16)]
    reduce_sum x3 -> x0, other arithmetic: 3.52 us -> none  [the longest x2 3.09 us: rms_norm(): mean_sq = jnp.mean(jnp.square(in_vec), axis=-1, keepdims=True)]
  transfers between devices with their start and end apart: 3 -> 0, of which waited for: 3 -> 0; matrix products, arithmetic and copies ran while one was open for 0% -> 0% of each run, Pallas kernels for 0% -> 0%
where the time goes in v1:
time: 90.3 us; the launch traced here: 89.6 us
  Pallas kernels  84.4 us (93%)
  other arithmetic  2.61 us (3%)
  local copies, waits for them, and re-layouts  1.97 us (2%)
    pallas_call x1, Pallas kernels, mix(): pl.pallas_call(mix_kernel, out_shape=jax.ShapeDtypeStruct((ROWS, DIM), BF...  66.1 us
    pallas_call x1, Pallas kernels, attend(): pl.pallas_call(attend_kernel, out_shape=(cache, cache, new, new, jax.Shap...  18.3 us
    unnamed x1, local copies, waits for them, and re-layouts  1.97 us

profile of v1, /device:TPU:1, one launch (start us, length us, event | category | flops | bytes accessed | tf_op | source)
XLA Modules:
  0.0 89.6 jit_solution(16037244457719254192)
XLA Ops:
  0.6 1.3 %reshape.48 = f32[5120]{0:T(1024)} convert(bf16[5120]{0:T(1024)(128)(2,1)} %param.18) | non-fusion elementwise | flops 5120 | bytes 30720 | tf_op jit(solution)/shard_map/reshape | solution.py:450
  1.9 1.3 %reshape.50 = f32[5120]{0:T(1024)} convert(bf16[5120]{0:T(1024)(128)(2,1)} %param.23) | non-fusion elementwise | flops 5120 | bytes 30720 | tf_op jit(solution)/shard_map/reshape | solution.py:452
  3.2 18.3 %attend.1 = (bf16[64,256,128]{2,1,0:T(8,128)(2,1)}, bf16[64,256,128]{2,1,0:T(8,128)(2,1)}, bf16[128,128]{1,0:T(8,128)(2,1)}, bf16[128,128]{1,0:T(8,128)(2,1)}, f32[2,264,128]{2,1,0:T(8,128)}) custom-call(s32[64]{0:T(128)} %pos_hbm.1, bf16[64,5120]{1,0:T(8,128)(2,1)} %x_hbm.3, f32[1,5120]{1,0:T(1,128)} %bitcast.11, f32[1,128]{1,0:T(1,128)} %constant.2.clone.freq_hbm, ...), custom_call_target="tpu_custom_call" | custom-call | tf_op jit(solution)/shard_map/attend/pallas_call | solution.py:157
  21.6 66.1 %mix.1 = bf16[64,5120]{1,0:T(8,128)(2,1)} custom-call(f32[2,264,128]{2,1,0:T(8,128)} %get-tuple-element.10.part_ref, bf16[64,5120]{1,0:T(8,128)(2,1)} %x_hbm.3, f32[1,5120]{1,0:T(1,128)} %bitcast.10, bf16[1024,5120]{1,0:T(8,128)(2,1)} %wo.1, bf16[5120,3584]{1,0:T(8,128)(2,1)} %wg.1, bf16[5120,3584]{1,0:T(8,128)(2,1)} %wu.1, bf16[3584,5120]{1,0:T(8,128)(2,1)} %wd.1), custom_call_target="tpu_custom_call" | custom-call | tf_op jit(solution)/shard_map/mix/pallas_call | solution.py:406
  87.6 2.0 %copy.20 = bf16[64,5120]{1,0:T(8,128)(2,1)} copy(bf16[64,5120]{1,0:T(8,128)(2,1)} %mix.1) | data formatting | bytes 1310720

commit v2 on v1

--- a/solution.py
+++ b/solution.py
@@ -13,8 +13,9 @@
 F32 = jnp.float32
 BF16 = jnp.bfloat16
 NEG = float(np.finfo(np.float32).min)
-VMEM_LIMIT = 62 * 1024 * 1024
-ANY = pl.BlockSpec(memory_space=pl.ANY)
+ATTEND_VMEM = 62 * 1024 * 1024
+MIX_VMEM = 48 * 1024 * 1024
+ANY = pl.BlockSpec(memory_space=pltpu.HBM)
 VM = pl.BlockSpec(memory_space=pltpu.VMEM)
 
 ROWS = 64
@@ -24,10 +25,11 @@
 KV = 2
 BLK = 128
 QKV = (HEADS + 2 * KV) * HD
-KSTEP = 512
+KSTEP = 1024
 KCH = DIM // KSTEP
 BCH = 8
 NB = ROWS // BCH
+LATE = 4
 
 
 def attend_kernel(pos_hbm, x_hbm, gain_hbm, freq_hbm, wq, wk, wv, kc, vc,
@@ -56,16 +58,12 @@
     for i in range(KCH):
         for cp in w_copies(i):
             cp.start()
-    for i in range(NB):
-        cache_copy(kc, k_v, sem_k, i).start()
-        cache_copy(vc, v_v, sem_v, i).start()
-
     for cp in small:
         cp.wait()
     for r in range(0, ROWS, 16):
         x = x_v[r:r + 16, :].astype(F32)
         inv = lax.rsqrt(jnp.mean(x * x, axis=-1, keepdims=True) + 1e-5)
-        n_v[r:r + 16, :] = (x * inv * gain_v[...].astype(F32)).astype(BF16)
+        n_v[r:r + 16, :] = (x * inv * gain_v[...].astype(F32).reshape(1, DIM)).astype(BF16)
     for b in range(ROWS):
         pos_v[b:b + 1, :] = jnp.full((1, HD), pos_s[b], jnp.int32)
     angles = pos_v[...].astype(F32) * freq_v[...]
@@ -79,6 +77,13 @@
     def w_step(i, carry):
         for cp in w_copies(i):
             cp.wait()
+        @pl.when(i >= KCH - LATE)
+        def _():
+            for u in range(NB // LATE):
+                at = (i - (KCH - LATE)) * (NB // LATE) + u
+                cache_copy(kc, k_v, sem_k, at).start()
+                cache_copy(vc, v_v, sem_v, at).start()
+
         rows = pl.ds(pl.multiple_of(i * KSTEP, KSTEP), KSTEP)
         acc[...] += jnp.dot(n_v[:, rows], w_v[rows, :], preferred_element_type=F32)
         return carry
@@ -162,7 +167,7 @@
         scratch_shapes=[
             pltpu.SMEM((ROWS,), jnp.int32),
             pltpu.VMEM((ROWS, DIM), BF16),
-            pltpu.VMEM((1, DIM), F32),
+            pltpu.VMEM((DIM,), BF16),
             pltpu.VMEM((1, HD), F32),
             pltpu.VMEM((DIM, QKV), BF16),
             pltpu.VMEM(kc.shape, BF16),
@@ -180,7 +185,7 @@
             pltpu.SemaphoreType.DMA((NB,)),
             pltpu.SemaphoreType.DMA((NB,)),
         ],
-        compiler_params=pltpu.CompilerParams(vmem_limit_bytes=VMEM_LIMIT),
+        compiler_params=pltpu.CompilerParams(vmem_limit_bytes=ATTEND_VMEM),
         name="attend",
     )(new_pos, x, gain, freq, wq, wk, wv, kc, vc)
 
@@ -337,7 +342,7 @@
     for r in range(0, ROWS, 16):
         h = hfull[r:r + 16, :]
         inv = lax.rsqrt(jnp.mean(h * h, axis=-1, keepdims=True) + 1e-5)
-        n2[r:r + 16, :] = (h * inv * gain_v[...].astype(F32)).astype(BF16)
+        n2[r:r + 16, :] = (h * inv * gain_v[...].astype(F32).reshape(1, DIM)).astype(BF16)
 
     def act_copies(j):
         own = act.at[sp, j]
@@ -410,7 +415,7 @@
         out_specs=VM,
         scratch_shapes=[
             pltpu.VMEM((RB, COLS), BF16),
-            pltpu.VMEM((1, DIM), F32),
+            pltpu.VMEM((DIM,), BF16),
             pltpu.VMEM((1024, COLS), BF16),
             pltpu.VMEM((HCH, DIM, 256), BF16),
             pltpu.VMEM((4, HID, COLS), BF16),
@@ -435,7 +440,7 @@
             dma((HCH,)), dma((HCH,)),
             dma((2, HCH)), dma((2, HCH)),
         ],
-        compiler_params=pltpu.CompilerParams(vmem_limit_bytes=VMEM_LIMIT, collective_id=0, has_side_effects=True),
+        compiler_params=pltpu.CompilerParams(vmem_limit_bytes=MIX_VMEM, collective_id=0, has_side_effects=True),
         name="mix",
     )(part, x, gain, wo, wg, wu, wd)
 
@@ -447,9 +452,9 @@
         freq = jnp.asarray(np.repeat(inv_freq, 2)[None, :])
         flat = (ROWS, BLK * KV, HD)
         k_out, v_out, k_new, v_new, part = attend(
-            new_pos, layer_in, attn_gain.astype(F32).reshape(1, DIM), freq, w_query, w_key, w_value,
+            new_pos, layer_in, attn_gain, freq, w_query, w_key, w_value,
             k_blk.reshape(flat), v_blk.reshape(flat))
-        layer_out = mix(part, layer_in, mlp_gain.astype(F32).reshape(1, DIM), w_out, w_gate, w_up, w_down)
+        layer_out = mix(part, layer_in, mlp_gain, w_out, w_gate, w_up, w_down)
         return (layer_out, k_out.reshape(k_blk.shape), v_out.reshape(v_blk.shape),
                 k_new.reshape(ROWS, KV, HD), v_new.reshape(ROWS, KV, HD))
 

time: 90.3 us -> 82.8 us (0.917)
  Pallas kernels: 84.4 us -> 80 us
  other arithmetic: 2.61 us -> 0 us
    pallas_call x1, Pallas kernels: 18.3 us -> 15.5 us  [attend(): pl.pallas_call(attend_kernel, out_shape=(cache, cache, new, new, jax.Shap...]
    reshape x2 -> x0, other arithmetic: 2.61 us -> none  [the longest x1 1.31 us: local_step(): attn_gain.astype(F32).reshape(1, DIM)]
    pallas_call x1, Pallas kernels: 66.1 us -> 64.6 us  [mix(): pl.pallas_call(mix_kernel, out_shape=jax.ShapeDtypeStruct((ROWS, DIM), BF...]
    unnamed x1 -> x7, local copies, waits for them, and re-layouts: 1.97 us -> 1.8 us
where the time goes in v2:
time: 82.8 us; the launch traced here: 82.5 us
  Pallas kernels  80 us (97%)
  local copies, waits for them, and re-layouts  1.8 us (2%)
    pallas_call x1, Pallas kernels, mix(): pl.pallas_call(mix_kernel, out_shape=jax.ShapeDtypeStruct((ROWS, DIM), BF...  64.6 us
    pallas_call x1, Pallas kernels, attend(): pl.pallas_call(attend_kernel, out_shape=(cache, cache, new, new, jax.Shap...  15.5 us
    unnamed x7, local copies, waits for them, and re-layouts  1.8 us

profile of v2, /device:TPU:1, one launch (start us, length us, event | category | flops | bytes accessed | tf_op | source)
XLA Modules:
  0.0 82.5 jit_solution(5336002923688874836)
XLA Ops:
  0.6 0.0 copy-start
  0.6 0.0 copy-start.2
  0.7 15.5 %attend.1 = (bf16[64,256,128]{2,1,0:T(8,128)(2,1)}, bf16[64,256,128]{2,1,0:T(8,128)(2,1)}, bf16[128,128]{1,0:T(8,128)(2,1)}, bf16[128,128]{1,0:T(8,128)(2,1)}, f32[2,264,128]{2,1,0:T(8,128)}) custom-call(s32[64]{0:T(128)} %pos_hbm.1, bf16[64,5120]{1,0:T(8,128)(2,1)} %x_hbm.3, bf16[5120]{0:T(1024)(128)(2,1)} %gain_hbm.2, f32[1,128]{1,0:T(1,128)} %constant.2.clone.freq_hbm, ...), custom_call_target="tpu_custom_call" | custom-call | tf_op jit(solution)/shard_map/attend/pallas_call | solution.py:162
  16.1 0.0 copy-done
  16.1 0.0 copy-done.2
  16.1 0.0 copy-start.1
  16.1 0.9 %copy-done.1 = f32[2,264,128]{2,1,0:T(8,128)S(1)} copy-done((f32[2,264,128]{2,1,0:T(8,128)S(1)}, f32[2,264,128]{2,1,0:T(8,128)}, u32[]{:S(2)}) %copy-start.1) | copy-done | bytes 270360
  17.1 64.6 %mix.1 = bf16[64,5120]{1,0:T(8,128)(2,1)S(1)} custom-call(f32[2,264,128]{2,1,0:T(8,128)S(1)} %copy-done.1, bf16[64,5120]{1,0:T(8,128)(2,1)S(1)} %copy-done, bf16[5120]{0:T(1024)(128)(2,1)S(1)} %copy-done.2, bf16[1024,5120]{1,0:T(8,128)(2,1)} %wo.1, bf16[5120,3584]{1,0:T(8,128)(2,1)} %wg.1, bf16[5120,3584]{1,0:T(8,128)(2,1)} %wu.1, bf16[3584,5120]{1,0:T(8,128)(2,1)} %wd.1), custom_call_target="tpu_custom_call" | custom-call | tf_op jit(solution)/shard_map/mix/pallas_call | solution.py:411
  81.7 0.8 %copy.20 = bf16[64,5120]{1,0:T(8,128)(2,1)} copy(bf16[64,5120]{1,0:T(8,128)(2,1)S(1)} %mix.1) | data formatting | bytes 1310720
Async XLA Ops:
  0.6 15.5 %copy-start = (bf16[64,5120]{1,0:T(8,128)(2,1)S(1)}, bf16[64,5120]{1,0:T(8,128)(2,1)}, u32[]{:S(2)}) copy-start(bf16[64,5120]{1,0:T(8,128)(2,1)} %x_hbm.3) | copy-start | bytes 1966084
  0.6 15.5 %copy-start.2 = (bf16[5120]{0:T(1024)(128)(2,1)S(1)}, bf16[5120]{0:T(1024)(128)(2,1)}, u32[]{:S(2)}) copy-start(bf16[5120]{0:T(1024)(128)(2,1)} %gain_hbm.3) | copy-start | bytes 30724
  16.1 1.0 %copy-start.1 = (f32[2,264,128]{2,1,0:T(8,128)S(1)}, f32[2,264,128]{2,1,0:T(8,128)}, u32[]{:S(2)}) copy-start(f32[2,264,128]{2,1,0:T(8,128)} %get-tuple-element.10.part_ref) | copy-start | bytes 811012

commit v3 on v2

--- a/solution.py
+++ b/solution.py
@@ -27,15 +27,16 @@
 QKV = (HEADS + 2 * KV) * HD
 KSTEP = 1024
 KCH = DIM // KSTEP
-BCH = 8
+BCH = 16
 NB = ROWS // BCH
+QROWS = BCH * HEADS
 LATE = 4
 
 
 def attend_kernel(pos_hbm, x_hbm, gain_hbm, freq_hbm, wq, wk, wv, kc, vc,
                   ko, vo, kn_ref, vn_ref, part_ref,
-                  pos_s, x_v, gain_v, freq_v, w_v, k_v, v_v, n_v, acc, pos_v, qs, ks, vs,
-                  sem_m, sem_w, sem_k, sem_v, sem_ko, sem_vo):
+                  pos_s, x_v, gain_v, freq_v, w_v, k_v, v_v, n_v, acc, pos_v, qs, ks, vs, kn_v, vn_v,
+                  sem_m, sem_w, sem_k, sem_v, sem_ko, sem_vo, sem_n):
     sp = lax.axis_index('sp')
 
     small = [pltpu.make_async_copy(pos_hbm, pos_s, sem_m.at[0]),
@@ -101,8 +102,11 @@
         ks[pl.ds(h, ROWS, stride=KV), :] = rotate(acc[:, lo:lo + HD])
         lo = (HEADS + KV + h) * HD
         vs[pl.ds(h, ROWS, stride=KV), :] = acc[:, lo:lo + HD].astype(BF16).astype(F32)
-    kn_ref[...] = ks[...].astype(BF16)
-    vn_ref[...] = vs[...].astype(BF16)
+    kn_v[...] = ks[...].astype(BF16)
+    vn_v[...] = vs[...].astype(BF16)
+    new_copies = [pltpu.make_async_copy(kn_v, kn_ref, sem_n.at[0]), pltpu.make_async_copy(vn_v, vn_ref, sem_n.at[1])]
+    for cp in new_copies:
+        cp.start()
 
     row16 = lax.broadcasted_iota(jnp.int32, (16, HD), 0)
     lane = lax.broadcasted_iota(jnp.int32, (HEADS, KV * BLK), 1)
@@ -120,7 +124,7 @@
         both = jnp.where(row16 % 2 == 0, new[pl.ds(2 * b, 1), :], new[pl.ds(2 * b + 1, 1), :])
         cache_v[b, at, :] = jnp.where(row16 // 2 == local, both, old).astype(BF16)
 
-    def chunk(i, stat):
+    for i in range(NB):
         cache_copy(kc, k_v, sem_k, i).wait()
         cache_copy(vc, v_v, sem_v, i).wait()
         slots = [pos_s[i * BCH + u] - sp * BLK for u in range(BCH)]
@@ -132,8 +136,9 @@
         raw = []
         for u in range(BCH):
             b = i * BCH + u
-            q = qs[pl.ds(pl.multiple_of(b * HEADS, HEADS), HEADS), :].astype(BF16)
+            q = qs[b * HEADS:(b + 1) * HEADS, :].astype(BF16)
             raw.append(lax.dot_general(q, k_v[b], (((1,), (1,)), ((), ())), preferred_element_type=F32))
+        stat = jnp.zeros((HEADS, HD), F32)
         for u in range(BCH):
             b = i * BCH + u
             valid = jnp.logical_and(same_head, lane_slot <= slots[u])
@@ -141,19 +146,15 @@
             top = jnp.max(score, axis=-1, keepdims=True)
             prob = jnp.where(valid, jnp.exp(score - top), 0.0)
             total = jnp.sum(prob, axis=-1, keepdims=True)
-            out = jnp.dot(prob.astype(BF16), v_v[b], preferred_element_type=F32)
-            half = b // 32
-            part_ref[half, pl.ds(pl.multiple_of((b - half * 32) * HEADS, HEADS), HEADS), :] = out
-            stat = jnp.where(stat_lane == b, top, stat)
-            stat = jnp.where(stat_lane == b + ROWS, total, stat)
-        return stat
-
-    stat = lax.fori_loop(0, NB, chunk, jnp.zeros((HEADS, HD), F32))
-    part_ref[0, 256:264, :] = stat
-    part_ref[1, 256:264, :] = pltpu.roll(stat, 96, 1)
+            part_ref[i, u * HEADS:(u + 1) * HEADS, :] = jnp.dot(prob.astype(BF16), v_v[b], preferred_element_type=F32)
+            stat = jnp.where(stat_lane == u, top, stat)
+            stat = jnp.where(stat_lane == u + 64, total, stat)
+        part_ref[i, QROWS:QROWS + HEADS, :] = stat
     for i in range(NB):
         cache_copy(k_v, ko, sem_ko, i).wait()
         cache_copy(v_v, vo, sem_vo, i).wait()
+    for cp in new_copies:
+        cp.wait()
 
 
 def attend(new_pos, x, gain, freq, wq, wk, wv, kc, vc):
@@ -161,9 +162,9 @@
     new = jax.ShapeDtypeStruct((ROWS * KV, HD), BF16)
     return pl.pallas_call(
         attend_kernel,
-        out_shape=(cache, cache, new, new, jax.ShapeDtypeStruct((2, 264, HD), F32)),
+        out_shape=(cache, cache, new, new, jax.ShapeDtypeStruct((NB, QROWS + HEADS, HD), F32)),
         in_specs=[ANY] * 9,
-        out_specs=(ANY, ANY, VM, VM, VM),
+        out_specs=(ANY,) * 4 + (VM,),
         scratch_shapes=[
             pltpu.SMEM((ROWS,), jnp.int32),
             pltpu.VMEM((ROWS, DIM), BF16),
@@ -178,12 +179,15 @@
             pltpu.VMEM((ROWS * HEADS, HD), F32),
             pltpu.VMEM((ROWS * KV, HD), F32),
             pltpu.VMEM((ROWS * KV, HD), F32),
+            pltpu.VMEM((ROWS * KV, HD), BF16),
+            pltpu.VMEM((ROWS * KV, HD), BF16),
             pltpu.SemaphoreType.DMA((4,)),
             pltpu.SemaphoreType.DMA((KCH, 3)),
             pltpu.SemaphoreType.DMA((NB,)),
             pltpu.SemaphoreType.DMA((NB,)),
             pltpu.SemaphoreType.DMA((NB,)),
             pltpu.SemaphoreType.DMA((NB,)),
+            pltpu.SemaphoreType.DMA((2,)),
         ],
         compiler_params=pltpu.CompilerParams(vmem_limit_bytes=ATTEND_VMEM),
         name="attend",
@@ -195,15 +199,15 @@
 HID = 896
 HCH = HID // 128
 RB = ROWS // TP
-NC = 2
-CW = COLS // NC
+CHUNKS = ((0, 512), (512, 768))
+NC = len(CHUNKS)
 
 
 def mix_kernel(part_ref, x_hbm, gain_hbm, wo, wg, wu, wd, out_ref,
                xb_v, gain_v, wo_v, wgu_v, wd_v,
                pa, pb, pc, at_o, lhs_v, mm, rs_buf, hfull, n2, act, act_b, ofull,
                sem_l, sem_g, sem_d, cs, cr, rs_s, rs_r, az_s, az_r, ay_s, ay_r, ac_s, ac_r,
-               my_s, my_r, mc_s, mc_r):
+               my_s, my_r, mc_s, mc_r, zr, gu_v):
     dp = lax.axis_index('dp')
     z = lax.axis_index('tp')
     sp = lax.axis_index('sp')
@@ -217,8 +221,11 @@
     dev_z = [None] + [(dp, lax.rem(z + d, TP), sp) for d in range(1, TP)]
     src_z = [z] + [lax.rem(z + TP - d, TP) for d in range(1, TP)]
 
-    def col_at(s, j=0, width=COLS):
-        return pl.ds(pl.multiple_of(s * COLS + j * width, 128), width)
+    def col_at(s):
+        return pl.ds(pl.multiple_of(s * COLS, 128), COLS)
+
+    def chunk_at(s, j):
+        return pl.ds(pl.multiple_of(s * COLS + CHUNKS[j][0], 128), CHUNKS[j][1])
 
     def row_at(zz):
         return pl.ds(pl.multiple_of(zz * RB, RB), RB)
@@ -243,10 +250,32 @@
     for cp in d_copies:
         cp.start()
 
+    has_l, has_r = z > 0, z < TP - 1
+    dev_l = (dp, jnp.maximum(z - 1, 0), sp)
+    dev_r = (dp, jnp.minimum(z + 1, TP - 1), sp)
+
+    def signal(sem, dev, cond=None):
+        if cond is None:
+            pl.semaphore_signal(sem, inc=1, device_id=dev, device_id_type=MESH)
+        else:
+            @pl.when(cond)
+            def _():
+                pl.semaphore_signal(sem, inc=1, device_id=dev, device_id_type=MESH)
+
+    def wait_if(sem, cond):
+        @pl.when(cond)
+        def _():
+            pl.semaphore_wait(sem, 1)
+
     barrier = pltpu.get_barrier_semaphore()
-    for dev in [dev_y, dev_c] + dev_z[1:]:
-        pl.semaphore_signal(barrier, inc=1, device_id=dev, device_id_type=MESH)
-    pl.semaphore_wait(barrier, 5)
+    signal(barrier, dev_y)
+    signal(barrier, dev_c)
+    signal(barrier, dev_l, has_l)
+    signal(barrier, dev_r, has_r)
+    pl.semaphore_wait(barrier, 2 + has_l.astype(jnp.int32) + has_r.astype(jnp.int32))
+    inner = jnp.logical_and(has_l, has_r)
+    signal(zr.at[0], dev_l, inner)
+    signal(zr.at[1], dev_r, inner)
 
     sends = []
 
@@ -266,30 +295,44 @@
         total = a1 * pltpu.roll(s1, 64, 1) + a2 * pltpu.roll(s2, 64, 1)
         return top, a1, a2, total
 
-    cp = push(part_ref.at[1 - c], pa, cs.at[0], cr.at[0], dev_c)
-    cp.wait_recv()
-    top, a1, a2, total = weights(part_ref[c, 256:264, :], pa[256:264, :])
-    for i in range(32):
-        r = slice(i * 8, i * 8 + 8)
-        pb[r, :] = a1[:, i:i + 1] * part_ref[c, r, :] + a2[:, i:i + 1] * pa[r, :]
-    pb[256:264, :] = jnp.where(lane < 64, top, pltpu.roll(total, 64, 1))
-    cp = push(pb, pc, cs.at[1], cr.at[1], dev_y)
-    cp.wait_recv()
-    top, a1, a2, total = weights(pb[256:264, :], pc[256:264, :])
-    a1 = a1 / total
-    a2 = a2 / total
     half = pl.multiple_of(c * 256, 256)
-    for i in range(32):
-        r = slice(i * 8, i * 8 + 8)
-        at_o[pl.ds(pl.multiple_of(half + i * 8, 8), 8), :] = a1[:, i:i + 1] * pb[r, :] + a2[:, i:i + 1] * pc[r, :]
-    mine = at_o.at[pl.ds(half, 256)]
-    cp = push(mine, mine, cs.at[2], cr.at[2], dev_c)
-    cp.wait_recv()
+    st = slice(QROWS, QROWS + HEADS)
+    first = [push(part_ref.at[(1 - c) * 2 + k], pa.at[k], cs.at[0, k], cr.at[0, k], dev_c) for k in range(2)]
+    second = []
+    for k in range(2):
+        first[k].wait_recv()
+        mine = part_ref.at[c * 2 + k]
+        top, a1, a2, total = weights(mine[st, :], pa[k, st, :])
+        for i in range(BCH):
+            r = slice(i * 8, i * 8 + 8)
+            pb[k, r, :] = a1[:, i:i + 1] * mine[r, :] + a2[:, i:i + 1] * pa[k, r, :]
+        pb[k, st, :] = jnp.where(lane < 64, top, pltpu.roll(total, 64, 1))
+        second.append(push(pb.at[k], pc.at[k], cs.at[1, k], cr.at[1, k], dev_y))
+    wait_if(zr.at[0], z + 2 < TP)
+    wait_if(zr.at[1], z - 2 >= 0)
+    signal(zr.at[2], dev_l, z == 1)
+    signal(zr.at[3], dev_r, z == 2)
+    third = []
+    for k in range(2):
+        second[k].wait_recv()
+        top, a1, a2, total = weights(pb[k, st, :], pc[k, st, :])
+        a1 = a1 / total
+        a2 = a2 / total
+        for i in range(BCH):
+            r = slice(i * 8, i * 8 + 8)
+            to = pl.ds(pl.multiple_of(half + k * QROWS + i * 8, 8), 8)
+            at_o[to, :] = a1[:, i:i + 1] * pb[k, r, :] + a2[:, i:i + 1] * pc[k, r, :]
+        piece = at_o.at[pl.ds(pl.multiple_of(half + k * QROWS, QROWS), QROWS)]
+        third.append(push(piece, piece, cs.at[2, k], cr.at[2, k], dev_c))
+    for cp in third:
+        cp.wait_recv()
+    wait_if(zr.at[2], z == 0)
+    wait_if(zr.at[3], z == TP - 1)
     for h in range(HEADS):
         lhs_v[:, h * HD:(h + 1) * HD] = at_o[pl.ds(h, ROWS, stride=HEADS), :].astype(BF16)
 
     def scatter(stage, j):
-        cols = pl.ds(j * CW, CW)
+        cols = pl.ds(*CHUNKS[j])
         for d in range(1, TP):
             zz = lax.rem(z + d, TP)
             push(mm.at[stage, row_at(zz), cols], rs_buf.at[stage, d - 1, :, cols],
@@ -297,19 +340,18 @@
 
     def gather(stage, base, full):
         def blk(s, d, j):
-            return full.at[row_at(src_z[d]), col_at(s, 0, COLS) if False else pl.ds(
-                pl.multiple_of(s * COLS + j * CW, 128), CW)]
+            return full.at[row_at(src_z[d]), chunk_at(s, j)]
 
         def wait_in(ref, sem):
             pltpu.make_async_copy(ref, ref, sem).wait()
 
         for j in range(NC):
-            cols = slice(j * CW, (j + 1) * CW)
+            cols = pl.ds(*CHUNKS[j])
             val = base(cols) + mm[stage, row_at(z), cols]
             for d in range(1, TP):
-                wait_in(rs_buf.at[stage, d - 1, :, pl.ds(j * CW, CW)], rs_r.at[stage, j, d - 1])
+                wait_in(rs_buf.at[stage, d - 1, :, cols], rs_r.at[stage, j, d - 1])
                 val = val + rs_buf[stage, d - 1, :, cols]
-            full[row_at(z), pl.ds(pl.multiple_of(sp * COLS + j * CW, 128), CW)] = val
+            full[row_at(z), chunk_at(sp, j)] = val
             own = blk(sp, 0, j)
             for d in range(1, TP):
                 push(own, own, az_s.at[stage, j, d - 1], az_r.at[stage, j, d - 1], dev_z[d])
@@ -334,7 +376,7 @@
     for cp in loads:
         cp.wait()
     for j in range(NC):
-        cols = slice(j * CW, (j + 1) * CW)
+        cols = pl.ds(*CHUNKS[j])
         mm[0, :, cols] = jnp.dot(lhs_v[...], wo_v[:, cols], preferred_element_type=F32)
         scatter(0, j)
     gather(0, lambda cols: xb_v[:, cols].astype(F32), hfull)
@@ -356,18 +398,23 @@
         return pltpu.make_async_remote_copy(src_ref=ref, dst_ref=ref, send_sem=mc_s.at[1, j], recv_sem=mc_r.at[1, j],
                                             device_id=dev_c, device_id_type=MESH)
 
-    def hidden_step(j, carry):
+    def hidden_dot(j):
         for cp in gu_copies(j):
             cp.wait()
-        gu = jnp.dot(n2[...], wgu_v[j], preferred_element_type=F32)
-        gate = gu[:, :128]
-        val = gate * jax.nn.sigmoid(gate) * gu[:, 128:]
+        gu_v[j % 2] = jnp.dot(n2[...], wgu_v[j], preferred_element_type=F32)
+
+    def hidden_act(j):
+        gate = gu_v[j % 2, :, :128]
+        val = gate * jax.nn.sigmoid(gate) * gu_v[j % 2, :, 128:]
         act[sp, j] = val.astype(BF16).astype(F32)
         for cp in act_copies(j):
             cp.start()
-        return carry
-
-    lax.fori_loop(0, HCH, hidden_step, 0)
+
+    hidden_dot(0)
+    for j in range(1, HCH):
+        hidden_dot(j)
+        hidden_act(j - 1)
+    hidden_act(HCH - 1)
 
     def down(i, s):
         for j in range(HCH):
@@ -379,6 +426,10 @@
                 mm[1, :, k:k + 256] = prod
             else:
                 mm[1, :, k:k + 256] += prod
+            if i == 3:
+                for j in range(NC):
+                    if CHUNKS[j][0] + CHUNKS[j][1] == k + 256:
+                        scatter(1, j)
 
     down(0, sp)
     for j in range(HCH):
@@ -391,8 +442,6 @@
     for j in range(HCH):
         fwd_copy(j).wait_recv()
     down(3, sp_yc)
-    for j in range(NC):
-        scatter(1, j)
 
     own_h = hfull.at[row_at(z), col_at(sp)]
     gather(1, lambda cols: own_h[:, cols], ofull)
@@ -419,9 +468,9 @@
             pltpu.VMEM((1024, COLS), BF16),
             pltpu.VMEM((HCH, DIM, 256), BF16),
             pltpu.VMEM((4, HID, COLS), BF16),
-            pltpu.VMEM((264, HD), F32),
-            pltpu.VMEM((264, HD), F32),
-            pltpu.VMEM((264, HD), F32),
+            pltpu.VMEM((2, QROWS + HEADS, HD), F32),
+            pltpu.VMEM((2, QROWS + HEADS, HD), F32),
+            pltpu.VMEM((2, QROWS + HEADS, HD), F32),
             pltpu.VMEM((ROWS * HEADS, HD), F32),
             pltpu.VMEM((ROWS, 1024), BF16),
             pltpu.VMEM((2, ROWS, COLS), F32),
@@ -432,13 +481,15 @@
             pltpu.VMEM((ROWS, HID), BF16),
             pltpu.VMEM((ROWS, DIM), F32),
             dma((3,)), dma((HCH, 2)), dma((4,)),
-            dma((3,)), dma((3,)),
+            dma((3, 2)), dma((3, 2)),
             dma((2, NC, 3)), dma((2, NC, 3)),
             dma((2, NC, 3)), dma((2, NC, 3)),
             dma((2, NC, TP)), dma((2, NC, TP)),
             dma((2, NC, 2 * TP)), dma((2, NC, 2 * TP)),
             dma((HCH,)), dma((HCH,)),
             dma((2, HCH)), dma((2, HCH)),
+            pltpu.SemaphoreType.REGULAR((4,)),
+            pltpu.VMEM((2, ROWS, 256), F32),
         ],
         compiler_params=pltpu.CompilerParams(vmem_limit_bytes=MIX_VMEM, collective_id=0, has_side_effects=True),
         name="mix",

time: 82.8 us -> 82.2 us (level)
    pallas_call x1, Pallas kernels: 15.5 us -> 14.2 us  [attend(): pl.pallas_call(attend_kernel, out_shape=(cache, cache, new, new, jax.Shap...]
where the time goes in v3:
time: 82.2 us; the launch traced here: 82 us
  Pallas kernels  79.5 us (97%)
  local copies, waits for them, and re-layouts  1.8 us (2%)
    pallas_call x1, Pallas kernels, mix(): pl.pallas_call(mix_kernel, out_shape=jax.ShapeDtypeStruct((ROWS, DIM), BF...  65.3 us
    pallas_call x1, Pallas kernels, attend(): pl.pallas_call(attend_kernel, out_shape=(cache, cache, new, new, jax.Shap...  14.2 us
    unnamed x7, local copies, waits for them, and re-layouts  1.8 us

profile of v3, /device:TPU:1, one launch (start us, length us, event | category | flops | bytes accessed | tf_op | source)
XLA Modules:
  0.0 82.0 jit_solution(17652583390082762069)
XLA Ops:
  0.6 0.0 copy-start
  0.6 0.0 copy-start.2
  0.7 14.2 %attend.1 = (bf16[64,256,128]{2,1,0:T(8,128)(2,1)}, bf16[64,256,128]{2,1,0:T(8,128)(2,1)}, bf16[128,128]{1,0:T(8,128)(2,1)}, bf16[128,128]{1,0:T(8,128)(2,1)}, f32[4,136,128]{2,1,0:T(8,128)}) custom-call(s32[64]{0:T(128)} %pos_hbm.1, bf16[64,5120]{1,0:T(8,128)(2,1)} %x_hbm.3, bf16[5120]{0:T(1024)(128)(2,1)} %gain_hbm.2, f32[1,128]{1,0:T(1,128)} %constant.2.clone.freq_hbm, ...), custom_call_target="tpu_custom_call" | custom-call | tf_op jit(solution)/shard_map/attend/pallas_call | solution.py:163
  14.9 0.0 copy-done
  14.9 0.0 copy-done.2
  14.9 0.0 copy-start.1
  14.9 0.9 %copy-done.1 = f32[4,136,128]{2,1,0:T(8,128)S(1)} copy-done((f32[4,136,128]{2,1,0:T(8,128)S(1)}, f32[4,136,128]{2,1,0:T(8,128)}, u32[]{:S(2)}) %copy-start.1) | copy-done | bytes 278552
  15.8 65.3 %mix.1 = bf16[64,5120]{1,0:T(8,128)(2,1)S(1)} custom-call(f32[4,136,128]{2,1,0:T(8,128)S(1)} %copy-done.1, bf16[64,5120]{1,0:T(8,128)(2,1)S(1)} %copy-done, bf16[5120]{0:T(1024)(128)(2,1)S(1)} %copy-done.2, bf16[1024,5120]{1,0:T(8,128)(2,1)} %wo.1, bf16[5120,3584]{1,0:T(8,128)(2,1)} %wg.1, bf16[5120,3584]{1,0:T(8,128)(2,1)} %wu.1, bf16[3584,5120]{1,0:T(8,128)(2,1)} %wd.1), custom_call_target="tpu_custom_call" | custom-call | tf_op jit(solution)/shard_map/mix/pallas_call | solution.py:460
  81.2 0.8 %copy.20 = bf16[64,5120]{1,0:T(8,128)(2,1)} copy(bf16[64,5120]{1,0:T(8,128)(2,1)S(1)} %mix.1) | data formatting | bytes 1310720
Async XLA Ops:
  0.6 14.2 %copy-start = (bf16[64,5120]{1,0:T(8,128)(2,1)S(1)}, bf16[64,5120]{1,0:T(8,128)(2,1)}, u32[]{:S(2)}) copy-start(bf16[64,5120]{1,0:T(8,128)(2,1)} %x_hbm.3) | copy-start | bytes 1966084
  0.6 14.2 %copy-start.2 = (bf16[5120]{0:T(1024)(128)(2,1)S(1)}, bf16[5120]{0:T(1024)(128)(2,1)}, u32[]{:S(2)}) copy-start(bf16[5120]{0:T(1024)(128)(2,1)} %gain_hbm.3) | copy-start | bytes 30724
  14.9 1.0 %copy-start.1 = (f32[4,136,128]{2,1,0:T(8,128)S(1)}, f32[4,136,128]{2,1,0:T(8,128)}, u32[]{:S(2)}) copy-start(f32[4,136,128]{2,1,0:T(8,128)} %get-tuple-element.10.part_ref) | copy-start | bytes 835588

commit v4 on v3

--- a/solution.py
+++ b/solution.py
@@ -13,10 +13,13 @@
 F32 = jnp.float32
 BF16 = jnp.bfloat16
 NEG = float(np.finfo(np.float32).min)
-ATTEND_VMEM = 62 * 1024 * 1024
+ATTEND_VMEM = 48 * 1024 * 1024
 MIX_VMEM = 48 * 1024 * 1024
 ANY = pl.BlockSpec(memory_space=pltpu.HBM)
 VM = pl.BlockSpec(memory_space=pltpu.VMEM)
+
+HALF_IDX = np.arange(64, dtype=np.float32)
+INV_FREQ = np.float32(1.0) / (np.float32(ROPE_THETA) ** (np.float32(2.0) * HALF_IDX / np.float32(128)))
 
 ROWS = 64
 DIM = 5120
@@ -30,19 +33,17 @@
 BCH = 16
 NB = ROWS // BCH
 QROWS = BCH * HEADS
-LATE = 4
-
-
-def attend_kernel(pos_hbm, x_hbm, gain_hbm, freq_hbm, wq, wk, wv, kc, vc,
+
+
+def attend_kernel(pos_hbm, x_hbm, gain_hbm, wq, wk, wv, kc, vc,
                   ko, vo, kn_ref, vn_ref, part_ref,
-                  pos_s, x_v, gain_v, freq_v, w_v, k_v, v_v, n_v, acc, pos_v, qs, ks, vs, kn_v, vn_v,
+                  pos_s, x_v, gain_v, w_v, k_v, v_v, n_v, acc, pos_v, qs, ks, vs, kn_v, vn_v,
                   sem_m, sem_w, sem_k, sem_v, sem_ko, sem_vo, sem_n):
     sp = lax.axis_index('sp')
 
     small = [pltpu.make_async_copy(pos_hbm, pos_s, sem_m.at[0]),
              pltpu.make_async_copy(x_hbm, x_v, sem_m.at[1]),
-             pltpu.make_async_copy(gain_hbm, gain_v, sem_m.at[2]),
-             pltpu.make_async_copy(freq_hbm, freq_v, sem_m.at[3])]
+             pltpu.make_async_copy(gain_hbm, gain_v, sem_m.at[2])]
     for cp in small:
         cp.start()
 
@@ -56,40 +57,47 @@
         rows = pl.ds(pl.multiple_of(i * BCH, BCH), BCH)
         return pltpu.make_async_copy(src.at[rows], dst.at[rows], sem.at[i])
 
-    for i in range(KCH):
+    def w_start(i):
         for cp in w_copies(i):
             cp.start()
+
+    def cache_start(i):
+        cache_copy(kc, k_v, sem_k, i).start()
+        cache_copy(vc, v_v, sem_v, i).start()
+
+    w_start(0)
     for cp in small:
         cp.wait()
+    w_start(1)
+    w_start(2)
     for r in range(0, ROWS, 16):
         x = x_v[r:r + 16, :].astype(F32)
         inv = lax.rsqrt(jnp.mean(x * x, axis=-1, keepdims=True) + 1e-5)
         n_v[r:r + 16, :] = (x * inv * gain_v[...].astype(F32).reshape(1, DIM)).astype(BF16)
     for b in range(ROWS):
         pos_v[b:b + 1, :] = jnp.full((1, HD), pos_s[b], jnp.int32)
-    angles = pos_v[...].astype(F32) * freq_v[...]
+    pair = lax.broadcasted_iota(jnp.int32, (8, HD), 1) // 2
+    freq = jnp.full((8, HD), float(INV_FREQ[0]), F32)
+    for i in range(1, HD // 2):
+        freq = jnp.where(pair == i, float(INV_FREQ[i]), freq)
+    angles = pos_v[...].astype(F32) * freq[0:1, :]
     cos_a = jnp.cos(angles)
     sin_a = jnp.sin(angles)
     odd = lax.broadcasted_iota(jnp.int32, (ROWS, HD), 1) % 2 == 1
     sin_a = jnp.where(odd, sin_a, -sin_a)
 
-    acc[...] = jnp.zeros_like(acc)
-
-    def w_step(i, carry):
+    after = {0: (3,), 1: (4, 5), 2: (6,), 3: (7,), 4: (8,)}
+    for i in range(KCH):
         for cp in w_copies(i):
             cp.wait()
-        @pl.when(i >= KCH - LATE)
-        def _():
-            for u in range(NB // LATE):
-                at = (i - (KCH - LATE)) * (NB // LATE) + u
-                cache_copy(kc, k_v, sem_k, at).start()
-                cache_copy(vc, v_v, sem_v, at).start()
-
-        rows = pl.ds(pl.multiple_of(i * KSTEP, KSTEP), KSTEP)
-        acc[...] += jnp.dot(n_v[:, rows], w_v[rows, :], preferred_element_type=F32)
-        return carry
-
-    lax.fori_loop(0, KCH, w_step, 0)
+        for nxt in after[i]:
+            if nxt < KCH:
+                w_start(nxt)
+            else:
+                cache_start(nxt - KCH)
+        rows = slice(i * KSTEP, (i + 1) * KSTEP)
+        prod = jnp.dot(n_v[:, rows], w_v[rows, :], preferred_element_type=F32)
+        acc[...] = prod if i == 0 else acc[...] + prod
 
     def rotate(val):
         swapped = jnp.where(odd, pltpu.roll(val, 1, 1), pltpu.roll(val, HD - 1, 1))
@@ -157,19 +165,19 @@
         cp.wait()
 
 
-def attend(new_pos, x, gain, freq, wq, wk, wv, kc, vc):
+def attend(new_pos, x, gain, wq, wk, wv, kc, vc):
+    args = [pltpu.with_memory_space_constraint(a, pltpu.HBM) for a in (new_pos, x, gain, wq, wk, wv, kc, vc)]
     cache = jax.ShapeDtypeStruct(kc.shape, BF16)
     new = jax.ShapeDtypeStruct((ROWS * KV, HD), BF16)
     return pl.pallas_call(
         attend_kernel,
         out_shape=(cache, cache, new, new, jax.ShapeDtypeStruct((NB, QROWS + HEADS, HD), F32)),
-        in_specs=[ANY] * 9,
+        in_specs=[ANY] * 8,
         out_specs=(ANY,) * 4 + (VM,),
         scratch_shapes=[
             pltpu.SMEM((ROWS,), jnp.int32),
             pltpu.VMEM((ROWS, DIM), BF16),
             pltpu.VMEM((DIM,), BF16),
-            pltpu.VMEM((1, HD), F32),
             pltpu.VMEM((DIM, QKV), BF16),
             pltpu.VMEM(kc.shape, BF16),
             pltpu.VMEM(vc.shape, BF16),
@@ -181,7 +189,7 @@
             pltpu.VMEM((ROWS * KV, HD), F32),
             pltpu.VMEM((ROWS * KV, HD), BF16),
             pltpu.VMEM((ROWS * KV, HD), BF16),
-            pltpu.SemaphoreType.DMA((4,)),
+            pltpu.SemaphoreType.DMA((3,)),
             pltpu.SemaphoreType.DMA((KCH, 3)),
             pltpu.SemaphoreType.DMA((NB,)),
             pltpu.SemaphoreType.DMA((NB,)),
@@ -191,7 +199,7 @@
         ],
         compiler_params=pltpu.CompilerParams(vmem_limit_bytes=ATTEND_VMEM),
         name="attend",
-    )(new_pos, x, gain, freq, wq, wk, wv, kc, vc)
+    )(*args)
 
 
 TP = 4
@@ -199,6 +207,9 @@
 HID = 896
 HCH = HID // 128
 RB = ROWS // TP
+SUMS = (1, 2, 3)
+SPREAD = (1, 3, 2)
+LAND = (1, 3, 2)
 CHUNKS = ((0, 512), (512, 768))
 NC = len(CHUNKS)
 
@@ -219,7 +230,8 @@
     dev_y = (dp, z, sp_y)
     dev_c = (dp, z, sp_c)
     dev_z = [None] + [(dp, lax.rem(z + d, TP), sp) for d in range(1, TP)]
-    src_z = [z] + [lax.rem(z + TP - d, TP) for d in range(1, TP)]
+
+    from_z = [z] + [lax.rem(z + TP - d, TP) for d in range(1, TP)]
 
     def col_at(s):
         return pl.ds(pl.multiple_of(s * COLS, 128), COLS)
@@ -241,14 +253,9 @@
         return (pltpu.make_async_copy(wg.at[:, cols], wgu_v.at[j, :, pl.ds(0, 128)], sem_g.at[j, 0]),
                 pltpu.make_async_copy(wu.at[:, cols], wgu_v.at[j, :, pl.ds(128, 128)], sem_g.at[j, 1]))
 
-    for j in range(HCH):
-        for cp in gu_copies(j):
-            cp.start()
     order = [sp, sp_c, sp_y, sp_yc]
     d_copies = [pltpu.make_async_copy(wd.at[pl.ds(pl.multiple_of(s * HID, 128), HID), col_at(sp)],
                                       wd_v.at[i], sem_d.at[i]) for i, s in enumerate(order)]
-    for cp in d_copies:
-        cp.start()
 
     has_l, has_r = z > 0, z < TP - 1
     dev_l = (dp, jnp.maximum(z - 1, 0), sp)
@@ -326,6 +333,11 @@
         third.append(push(piece, piece, cs.at[2, k], cr.at[2, k], dev_c))
     for cp in third:
         cp.wait_recv()
+    for j in range(HCH):
+        for cp in gu_copies(j):
+            cp.start()
+    for cp in d_copies:
+        cp.start()
     wait_if(zr.at[2], z == 0)
     wait_if(zr.at[3], z == TP - 1)
     for h in range(HEADS):
@@ -333,14 +345,14 @@
 
     def scatter(stage, j):
         cols = pl.ds(*CHUNKS[j])
-        for d in range(1, TP):
+        for d in SUMS:
             zz = lax.rem(z + d, TP)
             push(mm.at[stage, row_at(zz), cols], rs_buf.at[stage, d - 1, :, cols],
                  rs_s.at[stage, j, d - 1], rs_r.at[stage, j, d - 1], dev_z[d])
 
     def gather(stage, base, full):
         def blk(s, d, j):
-            return full.at[row_at(src_z[d]), chunk_at(s, j)]
+            return full.at[row_at(from_z[d]), chunk_at(s, j)]
 
         def wait_in(ref, sem):
             pltpu.make_async_copy(ref, ref, sem).wait()
@@ -353,18 +365,18 @@
                 val = val + rs_buf[stage, d - 1, :, cols]
             full[row_at(z), chunk_at(sp, j)] = val
             own = blk(sp, 0, j)
-            for d in range(1, TP):
+            for d in SPREAD:
                 push(own, own, az_s.at[stage, j, d - 1], az_r.at[stage, j, d - 1], dev_z[d])
             push(own, own, ay_s.at[stage, j, 0], ay_r.at[stage, j, 0], dev_y)
             push(own, own, ac_s.at[stage, j, 0], ac_r.at[stage, j, 0], dev_c)
         for j in range(NC):
-            for d in (1, 3, 2):
+            for d in LAND:
                 ref = blk(sp, d, j)
                 wait_in(ref, az_r.at[stage, j, d - 1])
                 push(ref, ref, ay_s.at[stage, j, d], ay_r.at[stage, j, d], dev_y)
                 push(ref, ref, ac_s.at[stage, j, d], ac_r.at[stage, j, d], dev_c)
         for j in range(NC):
-            for d in (0, 1, 3, 2):
+            for d in (0,) + LAND:
                 ref = blk(sp_y, d, j)
                 wait_in(ref, ay_r.at[stage, j, d])
                 push(ref, ref, ac_s.at[stage, j, TP + d], ac_r.at[stage, j, TP + d], dev_c)
@@ -398,9 +410,11 @@
         return pltpu.make_async_remote_copy(src_ref=ref, dst_ref=ref, send_sem=mc_s.at[1, j], recv_sem=mc_r.at[1, j],
                                             device_id=dev_c, device_id_type=MESH)
 
-    def hidden_dot(j):
+    for j in range(HCH):
         for cp in gu_copies(j):
             cp.wait()
+
+    def hidden_dot(j):
         gu_v[j % 2] = jnp.dot(n2[...], wgu_v[j], preferred_element_type=F32)
 
     def hidden_act(j):
@@ -498,12 +512,9 @@
 
 def solution(mesh):
     def local_step(layer_in, new_pos, k_blk, v_blk, attn_gain, w_query, w_key, w_value, w_out, mlp_gain, w_gate, w_up, w_down):
-        half_idx = np.arange(HD // 2, dtype=np.float32)
-        inv_freq = (1.0 / (np.float32(ROPE_THETA) ** (np.float32(2.0) * half_idx / np.float32(HD)))).astype(np.float32)
-        freq = jnp.asarray(np.repeat(inv_freq, 2)[None, :])
         flat = (ROWS, BLK * KV, HD)
         k_out, v_out, k_new, v_new, part = attend(
-            new_pos, layer_in, attn_gain, freq, w_query, w_key, w_value,
+            new_pos, layer_in, attn_gain, w_query, w_key, w_value,
             k_blk.reshape(flat), v_blk.reshape(flat))
         layer_out = mix(part, layer_in, mlp_gain, w_out, w_gate, w_up, w_down)
         return (layer_out, k_out.reshape(k_blk.shape), v_out.reshape(v_blk.shape),

time: 82.2 us -> 77.1 us (0.938)
  Pallas kernels: 79.5 us -> 75.4 us
  local copies, waits for them, and re-layouts: 1.8 us -> 0.85 us
    pallas_call x1, Pallas kernels: 14.2 us -> 12 us  [attend(): pl.pallas_call(attend_kernel, out_shape=(cache, cache, new, new, jax.Shap...]
    pallas_call x1, Pallas kernels: 65.3 us -> 63.3 us  [mix(): pl.pallas_call(mix_kernel, out_shape=jax.ShapeDtypeStruct((ROWS, DIM), BF...]
    unnamed x7 -> x5, local copies, waits for them, and re-layouts: 1.8 us -> 0.85 us
where the time goes in v4:
time: 77.1 us; the launch traced here: 76.9 us
  Pallas kernels  75.4 us (98%)
  local copies, waits for them, and re-layouts  0.85 us (1%)
    pallas_call x1, Pallas kernels, mix(): pl.pallas_call(mix_kernel, out_shape=jax.ShapeDtypeStruct((ROWS, DIM), BF...  63.3 us
    pallas_call x1, Pallas kernels, attend(): pl.pallas_call(attend_kernel, out_shape=(cache, cache, new, new, jax.Shap...  12 us

profile of v4, /device:TPU:1, one launch (start us, length us, event | category | flops | bytes accessed | tf_op | source)
XLA Modules:
  0.0 76.9 jit_solution(5346854562758640166)
XLA Ops:
  0.6 0.0 copy-start
  0.6 0.0 copy-start.1
  0.7 12.0 %attend.1 = (bf16[64,256,128]{2,1,0:T(8,128)(2,1)}, bf16[64,256,128]{2,1,0:T(8,128)(2,1)}, bf16[128,128]{1,0:T(8,128)(2,1)}, bf16[128,128]{1,0:T(8,128)(2,1)}, f32[4,136,128]{2,1,0:T(8,128)S(1)}) custom-call(s32[64]{0:T(128)} %pos_hbm.1, bf16[64,5120]{1,0:T(8,128)(2,1)} %x_hbm.3, bf16[5120]{0:T(1024)(128)(2,1)} %gain_hbm.2, bf16[5120,1024]{1,0:T(8,128)(2,1)} %wq.1, ...), custom_call_target="tpu_custom_call" | custom-call | tf_op jit(solution)/shard_map/attend/pallas_call | solution.py:172
  12.7 0.0 copy-done
  12.7 0.0 copy-done.1
  12.7 63.3 %mix.1 = bf16[64,5120]{1,0:T(8,128)(2,1)S(1)} custom-call(f32[4,136,128]{2,1,0:T(8,128)S(1)} %get-tuple-element.10.part_ref, bf16[64,5120]{1,0:T(8,128)(2,1)S(1)} %copy-done, bf16[5120]{0:T(1024)(128)(2,1)S(1)} %copy-done.1, bf16[1024,5120]{1,0:T(8,128)(2,1)} %wo.1, bf16[5120,3584]{1,0:T(8,128)(2,1)} %wg.1, bf16[5120,3584]{1,0:T(8,128)(2,1)} %wu.1, ...), custom_call_target="tpu_custom_call" | custom-call | tf_op jit(solution)/shard_map/mix/pallas_call | solution.py:474
  76.1 0.8 %copy.19 = bf16[64,5120]{1,0:T(8,128)(2,1)} copy(bf16[64,5120]{1,0:T(8,128)(2,1)S(1)} %mix.1) | data formatting | bytes 1310720
Async XLA Ops:
  0.6 12.1 %copy-start = (bf16[64,5120]{1,0:T(8,128)(2,1)S(1)}, bf16[64,5120]{1,0:T(8,128)(2,1)}, u32[]{:S(2)}) copy-start(bf16[64,5120]{1,0:T(8,128)(2,1)} %x_hbm.3) | copy-start | bytes 1966084
  0.6 12.1 %copy-start.1 = (bf16[5120]{0:T(1024)(128)(2,1)S(1)}, bf16[5120]{0:T(1024)(128)(2,1)}, u32[]{:S(2)}) copy-start(bf16[5120]{0:T(1024)(128)(2,1)} %gain_hbm.3) | copy-start | bytes 30724

commit v5 on v4

--- a/solution.py
+++ b/solution.py
@@ -86,7 +86,7 @@
     odd = lax.broadcasted_iota(jnp.int32, (ROWS, HD), 1) % 2 == 1
     sin_a = jnp.where(odd, sin_a, -sin_a)
 
-    after = {0: (3,), 1: (4, 5), 2: (6,), 3: (7,), 4: (8,)}
+    after = {0: (3,), 1: (4,), 2: (5, 6), 3: (7, 8), 4: ()}
     for i in range(KCH):
         for cp in w_copies(i):
             cp.wait()
@@ -206,11 +206,15 @@
 COLS = DIM // 4
 HID = 896
 HCH = HID // 128
+EXTRA = 3
+SENT = HCH - EXTRA
 RB = ROWS // TP
 SUMS = (1, 2, 3)
 SPREAD = (1, 3, 2)
 LAND = (1, 3, 2)
-CHUNKS = ((0, 512), (512, 768))
+RELAYED = (0, 1)
+NEAREST = (0, 1)
+CHUNKS = ((0, 512), (512, 256), (768, 512))
 NC = len(CHUNKS)
 
 
@@ -218,7 +222,7 @@
                xb_v, gain_v, wo_v, wgu_v, wd_v,
                pa, pb, pc, at_o, lhs_v, mm, rs_buf, hfull, n2, act, act_b, ofull,
                sem_l, sem_g, sem_d, cs, cr, rs_s, rs_r, az_s, az_r, ay_s, ay_r, ac_s, ac_r,
-               my_s, my_r, mc_s, mc_r, zr, gu_v):
+               my_s, my_r, mc_s, mc_r, zr, gu_v, zf_s):
     dp = lax.axis_index('dp')
     z = lax.axis_index('tp')
     sp = lax.axis_index('sp')
@@ -249,7 +253,8 @@
         cp.start()
 
     def gu_copies(j):
-        cols = pl.ds(pl.multiple_of(sp * HID + j * 128, 128), 128)
+        at = sp * HID + j * 128 if j < HCH else sp_y * HID + (j - EXTRA) * 128
+        cols = pl.ds(pl.multiple_of(at, 128), 128)
         return (pltpu.make_async_copy(wg.at[:, cols], wgu_v.at[j, :, pl.ds(0, 128)], sem_g.at[j, 0]),
                 pltpu.make_async_copy(wu.at[:, cols], wgu_v.at[j, :, pl.ds(128, 128)], sem_g.at[j, 1]))
 
@@ -333,7 +338,7 @@
         third.append(push(piece, piece, cs.at[2, k], cr.at[2, k], dev_c))
     for cp in third:
         cp.wait_recv()
-    for j in range(HCH):
+    for j in range(HCH + EXTRA):
         for cp in gu_copies(j):
             cp.start()
     for cp in d_copies:
@@ -350,9 +355,34 @@
             push(mm.at[stage, row_at(zz), cols], rs_buf.at[stage, d - 1, :, cols],
                  rs_s.at[stage, j, d - 1], rs_r.at[stage, j, d - 1], dev_z[d])
 
+    mate = z + 1 - 2 * lax.rem(z, 2)
+    cross = jnp.where(z < 2, 2, 1)
+    near = [z, jnp.where(z < 2, z + 1, z - 1),
+            jnp.where(z == 0, 2, jnp.where(z == TP - 1, 1, mate)),
+            jnp.where(z < 2, TP - 1, 0)]
+
+    def source(j, k):
+        return near[k] if j in NEAREST else from_z[((0,) + LAND)[k]]
+
+    def relay(stage, j, src, start):
+        full = ofull if stage else hfull
+        ref = full.at[row_at(src), chunk_at(sp, j)]
+
+        @pl.when(jnp.logical_and(inner, src // 2 != z // 2))
+        def _():
+            to = lax.rem(mate - src + TP, TP) - 1
+            cp = pltpu.make_async_remote_copy(src_ref=ref, dst_ref=ref,
+                                              send_sem=zf_s.at[stage, j, lax.rem(z - src + TP, TP) - 1],
+                                              recv_sem=az_r.at[stage, j, to], device_id=(dp, mate, sp),
+                                              device_id_type=MESH)
+            if start:
+                cp.start()
+            else:
+                cp.wait_send()
+
     def gather(stage, base, full):
-        def blk(s, d, j):
-            return full.at[row_at(from_z[d]), chunk_at(s, j)]
+        def blk(s, k, j):
+            return full.at[row_at(source(j, k)), chunk_at(s, j)]
 
         def wait_in(ref, sem):
             pltpu.make_async_copy(ref, ref, sem).wait()
@@ -365,18 +395,24 @@
                 val = val + rs_buf[stage, d - 1, :, cols]
             full[row_at(z), chunk_at(sp, j)] = val
             own = blk(sp, 0, j)
-            for d in SPREAD:
-                push(own, own, az_s.at[stage, j, d - 1], az_r.at[stage, j, d - 1], dev_z[d])
+            if j in RELAYED:
+                push(own, own, az_s.at[stage, j, 0], az_r.at[stage, j, lax.rem(cross - z + TP, TP) - 1], (dp, cross, sp))
+                push(own, own, az_s.at[stage, j, 1], az_r.at[stage, j, lax.rem(mate - z + TP, TP) - 1], (dp, mate, sp))
+            else:
+                for d in SPREAD:
+                    push(own, own, az_s.at[stage, j, d - 1], az_r.at[stage, j, d - 1], dev_z[d])
             push(own, own, ay_s.at[stage, j, 0], ay_r.at[stage, j, 0], dev_y)
             push(own, own, ac_s.at[stage, j, 0], ac_r.at[stage, j, 0], dev_c)
         for j in range(NC):
-            for d in LAND:
+            for d in range(1, TP):
                 ref = blk(sp, d, j)
-                wait_in(ref, az_r.at[stage, j, d - 1])
+                wait_in(ref, az_r.at[stage, j, lax.rem(z - source(j, d) + TP, TP) - 1])
+                if j in RELAYED:
+                    relay(stage, j, source(j, d), True)
                 push(ref, ref, ay_s.at[stage, j, d], ay_r.at[stage, j, d], dev_y)
                 push(ref, ref, ac_s.at[stage, j, d], ac_r.at[stage, j, d], dev_c)
         for j in range(NC):
-            for d in (0,) + LAND:
+            for d in range(TP):
                 ref = blk(sp_y, d, j)
                 wait_in(ref, ay_r.at[stage, j, d])
                 push(ref, ref, ac_s.at[stage, j, TP + d], ac_r.at[stage, j, TP + d], dev_c)
@@ -410,7 +446,7 @@
         return pltpu.make_async_remote_copy(src_ref=ref, dst_ref=ref, send_sem=mc_s.at[1, j], recv_sem=mc_r.at[1, j],
                                             device_id=dev_c, device_id_type=MESH)
 
-    for j in range(HCH):
+    for j in range(HCH + EXTRA):
         for cp in gu_copies(j):
             cp.wait()
 
@@ -419,16 +455,22 @@
 
     def hidden_act(j):
         gate = gu_v[j % 2, :, :128]
-        val = gate * jax.nn.sigmoid(gate) * gu_v[j % 2, :, 128:]
-        act[sp, j] = val.astype(BF16).astype(F32)
-        for cp in act_copies(j):
-            cp.start()
+        val = (gate * jax.nn.sigmoid(gate) * gu_v[j % 2, :, 128:]).astype(BF16).astype(F32)
+        if j < HCH:
+            act[sp, j] = val
+            to_y, to_c = act_copies(j)
+            if j < SENT:
+                to_y.start()
+            to_c.start()
+        else:
+            act[sp_y, j - EXTRA] = val
+            fwd_copy(j - EXTRA).start()
 
     hidden_dot(0)
-    for j in range(1, HCH):
+    for j in range(1, HCH + EXTRA):
         hidden_dot(j)
         hidden_act(j - 1)
-    hidden_act(HCH - 1)
+    hidden_act(HCH + EXTRA - 1)
 
     def down(i, s):
         for j in range(HCH):
@@ -449,7 +491,7 @@
     for j in range(HCH):
         act_copies(j)[1].wait_recv()
     down(1, sp_c)
-    for j in range(HCH):
+    for j in range(SENT):
         act_copies(j)[0].wait_recv()
         fwd_copy(j).start()
     down(2, sp_y)
@@ -463,9 +505,15 @@
 
     for cp in sends:
         cp.wait_send()
+    for stage in range(2):
+        for j in RELAYED:
+            for d in range(1, TP):
+                relay(stage, j, source(j, d), False)
     for j in range(HCH):
-        for cp in act_copies(j):
-            cp.wait_send()
+        to_y, to_c = act_copies(j)
+        if j < SENT:
+            to_y.wait_send()
+        to_c.wait_send()
         fwd_copy(j).wait_send()
 
 
@@ -480,7 +528,7 @@
             pltpu.VMEM((RB, COLS), BF16),
             pltpu.VMEM((DIM,), BF16),
             pltpu.VMEM((1024, COLS), BF16),
-            pltpu.VMEM((HCH, DIM, 256), BF16),
+            pltpu.VMEM((HCH + EXTRA, DIM, 256), BF16),
             pltpu.VMEM((4, HID, COLS), BF16),
             pltpu.VMEM((2, QROWS + HEADS, HD), F32),
             pltpu.VMEM((2, QROWS + HEADS, HD), F32),
@@ -494,7 +542,7 @@
             pltpu.VMEM((4, HCH, ROWS, 128), F32),
             pltpu.VMEM((ROWS, HID), BF16),
             pltpu.VMEM((ROWS, DIM), F32),
-            dma((3,)), dma((HCH, 2)), dma((4,)),
+            dma((3,)), dma((HCH + EXTRA, 2)), dma((4,)),
             dma((3, 2)), dma((3, 2)),
             dma((2, NC, 3)), dma((2, NC, 3)),
             dma((2, NC, 3)), dma((2, NC, 3)),
@@ -504,6 +552,7 @@
             dma((2, HCH)), dma((2, HCH)),
             pltpu.SemaphoreType.REGULAR((4,)),
             pltpu.VMEM((2, ROWS, 256), F32),
+            dma((2, NC, 3)),
         ],
         compiler_params=pltpu.CompilerParams(vmem_limit_bytes=MIX_VMEM, collective_id=0, has_side_effects=True),
         name="mix",

time: 77.1 us -> 75.7 us (0.982)
  Pallas kernels: 75.4 us -> 74.1 us
    pallas_call x1, Pallas kernels: 63.3 us -> 62 us  [mix(): pl.pallas_call(mix_kernel, out_shape=jax.ShapeDtypeStruct((ROWS, DIM), BF...]
where the time goes in v5:
time: 75.7 us; the launch traced here: 75.6 us
  Pallas kernels  74.1 us (98%)
  local copies, waits for them, and re-layouts  0.85 us (1%)
    pallas_call x1, Pallas kernels, mix(): pl.pallas_call(mix_kernel, out_shape=jax.ShapeDtypeStruct((ROWS, DIM), BF...  62 us
    pallas_call x1, Pallas kernels, attend(): pl.pallas_call(attend_kernel, out_shape=(cache, cache, new, new, jax.Shap...  12 us

profile of v5, /device:TPU:1, one launch (start us, length us, event | category | flops | bytes accessed | tf_op | source)
XLA Modules:
  0.0 75.6 jit_solution(4952313724919905885)
XLA Ops:
  0.6 0.0 copy-start
  0.6 0.0 copy-start.1
  0.7 12.0 %attend.1 = (bf16[64,256,128]{2,1,0:T(8,128)(2,1)}, bf16[64,256,128]{2,1,0:T(8,128)(2,1)}, bf16[128,128]{1,0:T(8,128)(2,1)}, bf16[128,128]{1,0:T(8,128)(2,1)}, f32[4,136,128]{2,1,0:T(8,128)S(1)}) custom-call(s32[64]{0:T(128)} %pos_hbm.1, bf16[64,5120]{1,0:T(8,128)(2,1)} %x_hbm.3, bf16[5120]{0:T(1024)(128)(2,1)} %gain_hbm.2, bf16[5120,1024]{1,0:T(8,128)(2,1)} %wq.1, ...), custom_call_target="tpu_custom_call" | custom-call | tf_op jit(solution)/shard_map/attend/pallas_call | solution.py:172
  12.7 0.0 copy-done
  12.7 0.0 copy-done.1
  12.7 62.0 %mix.1 = bf16[64,5120]{1,0:T(8,128)(2,1)S(1)} custom-call(f32[4,136,128]{2,1,0:T(8,128)S(1)} %get-tuple-element.10.part_ref, bf16[64,5120]{1,0:T(8,128)(2,1)S(1)} %copy-done, bf16[5120]{0:T(1024)(128)(2,1)S(1)} %copy-done.1, bf16[1024,5120]{1,0:T(8,128)(2,1)} %wo.1, bf16[5120,3584]{1,0:T(8,128)(2,1)} %wg.1, bf16[5120,3584]{1,0:T(8,128)(2,1)} %wu.1, ...), custom_call_target="tpu_custom_call" | custom-call | tf_op jit(solution)/shard_map/mix/pallas_call | solution.py:522
  74.7 0.8 %copy.19 = bf16[64,5120]{1,0:T(8,128)(2,1)} copy(bf16[64,5120]{1,0:T(8,128)(2,1)S(1)} %mix.1) | data formatting | bytes 1310720
Async XLA Ops:
  0.6 12.1 %copy-start = (bf16[64,5120]{1,0:T(8,128)(2,1)S(1)}, bf16[64,5120]{1,0:T(8,128)(2,1)}, u32[]{:S(2)}) copy-start(bf16[64,5120]{1,0:T(8,128)(2,1)} %x_hbm.3) | copy-start | bytes 1966084
  0.6 12.1 %copy-start.1 = (bf16[5120]{0:T(1024)(128)(2,1)S(1)}, bf16[5120]{0:T(1024)(128)(2,1)}, u32[]{:S(2)}) copy-start(bf16[5120]{0:T(1024)(128)(2,1)} %gain_hbm.3) | copy-start | bytes 30724
